TPU v7x, 32 devices: a whole 2x2x4 slice. The times are simulated.
32 devices in a mesh: dp: 4 (over x, core), seq: 2 (over y), tensor: 4 (over z).
Axes of the slice: x: 2, y: 2, z: 4, core: 2. Of those that a mesh axis runs over, the one named last changes fastest.
Arguments:
- inputs: bfloat16 [4, 2, 1024, 1536], P('dp', None, 'seq'), may hold values from -6 to 6
- segment_ids: int32 [4, 2, 1024], P('dp'), may hold values from 0 to 6, as said below
- ancestry: int32 [4, 2, 7, 7], P('dp'), may hold values from 0 to 1, as said below
- w_query: bfloat16 [1536, 1536], P(None, 'tensor'), may hold values from -0.15625 to 0.15625
- key_weight: bfloat16 [1536, 768], P(None, 'tensor'), may hold values from -0.15625 to 0.15625
- value_weight: bfloat16 [1536, 768], P(None, 'tensor'), may hold values from -0.15625 to 0.15625
- w_output: bfloat16 [1536, 1536], P('tensor'), may hold values from -0.875 to 0.875
- w_gate: bfloat16 [1536, 4096], P(None, 'tensor'), may hold values from -0.15625 to 0.15625
- w_up: bfloat16 [1536, 4096], P(None, 'tensor'), may hold values from -0.15625 to 0.15625
- w_down: bfloat16 [4096, 1536], P('tensor'), may hold values from -0.09375 to 0.09375
- attn_gain: float32 [1536], replicated, may hold values from 0.5 to 1.5
- ffn_gain: float32 [1536], replicated, may hold values from 0.5 to 1.5
- cotangent: bfloat16 [4, 2, 1024, 1536], P('dp', None, 'seq'), may hold values from -6 to 6
- mom_query: float32 [1536, 1536], P(('dp', 'seq'), 'tensor'), may hold values from -12 to 12
- key_momentum: float32 [1536, 768], P(('dp', 'seq'), 'tensor'), may hold values from -12 to 12
- value_momentum: float32 [1536, 768], P(('dp', 'seq'), 'tensor'), may hold values from -12 to 12
- mom_output: float32 [1536, 1536], P('tensor', ('dp', 'seq')), may hold values from -12 to 12
- mom_gate: float32 [1536, 4096], P(('dp', 'seq'), 'tensor'), may hold values from -12 to 12
- mom_up: float32 [1536, 4096], P(('dp', 'seq'), 'tensor'), may hold values from -12 to 12
- mom_down: float32 [4096, 1536], P('tensor', ('dp', 'seq')), may hold values from -12 to 12
- attn_first: float32 [1536], replicated, may hold values from -30 to 30
- attn_second: float32 [1536], replicated, may hold values from 50 to 500
- ffn_first: float32 [1536], replicated, may hold values from -30 to 30
- ffn_second: float32 [1536], replicated, may hold values from 50 to 500
Outputs:
- block_out: float32 [4, 2, 1024, 1536], P('dp', None, 'seq')
- input_grad: float32 [4, 2, 1024, 1536], P('dp', None, 'seq')
- grad_query: float32 [1536, 1536], P(('dp', 'seq'), 'tensor')
- grad_key: float32 [1536, 768], P(('dp', 'seq'), 'tensor')
- grad_value: float32 [1536, 768], P(('dp', 'seq'), 'tensor')
- grad_output: float32 [1536, 1536], P('tensor', ('dp', 'seq'))
- grad_gate: float32 [1536, 4096], P(('dp', 'seq'), 'tensor')
- grad_up: float32 [1536, 4096], P(('dp', 'seq'), 'tensor')
- grad_down: float32 [4096, 1536], P('tensor', ('dp', 'seq'))
- attn_gain_grad: float32 [1536], replicated
- ffn_gain_grad: float32 [1536], replicated
- new_mom_query: float32 [1536, 1536], P(('dp', 'seq'), 'tensor')
- new_mom_key: float32 [1536, 768], P(('dp', 'seq'), 'tensor')
- new_mom_value: float32 [1536, 768], P(('dp', 'seq'), 'tensor')
- new_mom_output: float32 [1536, 1536], P('tensor', ('dp', 'seq'))
- new_mom_gate: float32 [1536, 4096], P(('dp', 'seq'), 'tensor')
- new_mom_up: float32 [1536, 4096], P(('dp', 'seq'), 'tensor')
- new_mom_down: float32 [4096, 1536], P('tensor', ('dp', 'seq'))
- step_query: float32 [1536, 1536], P(('dp', 'seq'), 'tensor')
- step_key: float32 [1536, 768], P(('dp', 'seq'), 'tensor')
- step_value: float32 [1536, 768], P(('dp', 'seq'), 'tensor')
- step_output: float32 [1536, 1536], P('tensor', ('dp', 'seq'))
- step_gate: float32 [1536, 4096], P(('dp', 'seq'), 'tensor')
- step_up: float32 [1536, 4096], P(('dp', 'seq'), 'tensor')
- step_down: float32 [4096, 1536], P('tensor', ('dp', 'seq'))
- attn_first_new: float32 [1536], replicated
- attn_second_new: float32 [1536], replicated
- attn_gain_step: float32 [1536], replicated
- ffn_first_new: float32 [1536], replicated
- ffn_second_new: float32 [1536], replicated
- ffn_gain_step: float32 [1536], replicated
Inputs may be any that keep to these rules, and one draw needn't show every extreme that they name: `segment_ids`: in every tree: a trunk segment of 512 tokens comes first; two branch segments of 128 tokens hang from it and two leaf segments of 64 tokens from each branch; every segment lies in one run of positions after all of its ancestors; the 7 labels are distinct and their assignment varies. ancestry[., ., a, b] is 1 where segment b is segment a or one of its ancestors in that tree, else 0.
All inputs are finite; a program needn't handle non-finite values.
Results may differ from a plain program's by a relative error of at most 0.023.
Values may be sent and summed in bfloat16 or wider, within the bound.
A program may use at most 256 MiB of HBM per device.

v0:
```python
import math

import jax
import jax.numpy as jnp
from jax import lax
from jax.sharding import PartitionSpec as P

MODEL_WIDTH = 1536
HEAD_SIZE = 96
ITERS_NS = 3
ADAM_STEP = 10


HIGH = lax.Precision.HIGHEST
EPS_NORM = 1e-05
ROPE_THETA = 100000.0
MU_MUON = 0.95
NS_A = 3.4445
NS_B = -4.775
NS_C = 2.0315
LR_MUON = 0.1
EPS_MUON = 1e-07
BETA_ONE = 0.9
BETA_TWO = 0.95
LR_ADAM = 0.01
EPS_ADAM = 1e-08


def rms_scale(values):
    return lax.rsqrt(jnp.mean(values * values, axis=-1, keepdims=True) + EPS_NORM)


def norm_back(upstream, plain, scale, gain):
    scaled = upstream * gain
    return scale * (scaled - plain * jnp.mean(scaled * plain, axis=-1, keepdims=True))


def rotary_tables(positions):
    half = HEAD_SIZE // 2
    freq = jnp.power(ROPE_THETA, -(2.0 * jnp.arange(half, dtype=jnp.float32)) / HEAD_SIZE)
    angle = positions[..., None] * freq
    return (jnp.cos(angle), jnp.sin(angle))


def rotary(values, cosine, sine):
    shape = values.shape
    heads = values.reshape(shape[:-1] + (shape[-1] // HEAD_SIZE, HEAD_SIZE))
    half = HEAD_SIZE // 2
    front = heads[..., :half]
    back = heads[..., half:]
    cos_h = cosine[..., None, :]
    sin_h = sine[..., None, :]
    return jnp.concatenate(
        [front * cos_h - back * sin_h, back * cos_h + front * sin_h], axis=-1
    ).reshape(shape)


def rotary_back(values, cosine, sine):
    shape = values.shape
    heads = values.reshape(shape[:-1] + (shape[-1] // HEAD_SIZE, HEAD_SIZE))
    half = HEAD_SIZE // 2
    front = heads[..., :half]
    back = heads[..., half:]
    cos_h = cosine[..., None, :]
    sin_h = sine[..., None, :]
    return jnp.concatenate(
        [front * cos_h + back * sin_h, back * cos_h - front * sin_h], axis=-1
    ).reshape(shape)


def outer_sum(left, right):
    return jnp.einsum("ta,tb->ab", left, right, preferred_element_type=jnp.float32)


def gram_pieces(matrix):
    half = matrix.shape[1] // 2
    front = matrix[:, :half]
    back = matrix[:, half:]
    return jnp.stack(
        [
            jnp.dot(front.T, front, precision=HIGH),
            jnp.dot(front.T, back, precision=HIGH),
            jnp.dot(back.T, back, precision=HIGH),
        ]
    )


def gram_join(pieces):
    upper = jnp.concatenate([pieces[0], pieces[1]], axis=1)
    lower = jnp.concatenate([pieces[1].T, pieces[2]], axis=1)
    return jnp.concatenate([upper, lower], axis=0)


def newton_step(ortho, gram):
    poly = NS_B * gram + NS_C * jnp.dot(gram, gram, precision=HIGH)
    return NS_A * ortho + jnp.dot(ortho, poly, precision=HIGH)


def adam(grad, first, second):
    first_new = BETA_ONE * first + (1.0 - BETA_ONE) * grad
    second_new = BETA_TWO * second + (1.0 - BETA_TWO) * grad * grad
    corrected = first_new / (1.0 - BETA_ONE**ADAM_STEP)
    spread = jnp.sqrt(second_new / (1.0 - BETA_TWO**ADAM_STEP)) + EPS_ADAM
    return (first_new, second_new, -LR_ADAM * corrected / spread)


def shards(
    inputs,
    segment_ids,
    ancestry,
    w_query,
    key_weight,
    value_weight,
    w_output,
    w_gate,
    w_up,
    w_down,
    attn_gain,
    ffn_gain,
    cotangent,
    mom_query,
    key_momentum,
    value_momentum,
    mom_output,
    mom_gate,
    mom_up,
    mom_down,
    attn_first,
    attn_second,
    ffn_first,
    ffn_second,
):
    tokens_local = inputs.shape[2]
    tree_len = segment_ids.shape[2]
    seg_count = ancestry.shape[2]
    width = inputs.shape[3]
    q_width = w_query.shape[1]
    kv_width = key_weight.shape[1]
    ff_width = w_gate.shape[1]
    kv_heads = kv_width // HEAD_SIZE
    group = q_width // kv_width
    scale = 1.0 / math.sqrt(HEAD_SIZE)
    start = lax.axis_index("seq") * tokens_local
    query_index = start + jnp.arange(tokens_local, dtype=jnp.int32)
    key_index = jnp.arange(tree_len, dtype=jnp.int32)
    labels = jnp.arange(seg_count, dtype=jnp.int32)

    def scores_of(query_rot, key_all):
        query_heads = query_rot.reshape(tokens_local, kv_heads, group, HEAD_SIZE)
        key_heads = key_all.reshape(tree_len, kv_heads, HEAD_SIZE)
        return (
            jnp.einsum("tkgd,skd->kgts", query_heads, key_heads, preferred_element_type=jnp.float32)
            * scale
        )

    def micro(carry, batch):
        grads, gain_one, gain_two = carry
        block_in, block_cot, seg_tree, anc_tree = batch
        member_all = (seg_tree[:, None] == labels[None, :]).astype(jnp.float32)
        member_own = lax.dynamic_slice_in_dim(member_all, start, tokens_local, 0)
        reach = jnp.dot(member_own, anc_tree.astype(jnp.float32))
        on_path = jnp.dot(reach, member_all.T) > 0.5
        allowed = on_path & (query_index[:, None] >= key_index[None, :])
        positions = (jnp.sum(allowed.astype(jnp.int32), axis=1) - 1).astype(jnp.float32)
        cosine, sine = rotary_tables(positions)
        resid = block_in.astype(jnp.float32)
        scale_one = rms_scale(resid)
        plain_one = resid * scale_one
        normed_one = (plain_one * attn_gain).astype(jnp.bfloat16)
        query_rot = rotary(
            jnp.dot(normed_one, w_query, preferred_element_type=jnp.float32), cosine, sine
        ).astype(jnp.bfloat16)
        key_rot = rotary(
            jnp.dot(normed_one, key_weight, preferred_element_type=jnp.float32), cosine, sine
        ).astype(jnp.bfloat16)
        value_own = jnp.dot(normed_one, value_weight, preferred_element_type=jnp.float32).astype(
            jnp.bfloat16
        )
        key_all, value_all = (
            lax.all_gather(key_rot, "seq", axis=0, tiled=True),
            lax.all_gather(value_own, "seq", axis=0, tiled=True),
        )
        masked = jnp.where(allowed[None, None], scores_of(query_rot, key_all), -1e30)
        top = jnp.max(masked, axis=-1, keepdims=True)
        expo = jnp.exp(masked - top)
        total = jnp.sum(expo, axis=-1, keepdims=True)
        logsum = top + jnp.log(total)
        probs = (expo / total).astype(jnp.bfloat16)
        value_heads = value_all.reshape(tree_len, kv_heads, HEAD_SIZE)
        mixed = (
            jnp.einsum("kgts,skd->tkgd", probs, value_heads, preferred_element_type=jnp.float32)
            .reshape(tokens_local, q_width)
            .astype(jnp.bfloat16)
        )
        attn_out = lax.psum(jnp.dot(mixed, w_output, preferred_element_type=jnp.float32), "tensor")
        middle = resid + attn_out
        scale_two = rms_scale(middle)
        plain_two = middle * scale_two
        normed_two = (plain_two * ffn_gain).astype(jnp.bfloat16)
        gate = jnp.dot(normed_two, w_gate, preferred_element_type=jnp.float32)
        up_value = jnp.dot(normed_two, w_up, preferred_element_type=jnp.float32)
        sigma = jax.nn.sigmoid(gate)
        active = gate * sigma
        inner = (active * up_value).astype(jnp.bfloat16)
        ffn_out = lax.psum(
            jnp.dot(inner, w_down, preferred_element_type=jnp.float32).astype(jnp.bfloat16),
            "tensor",
        ).astype(jnp.float32)
        block_out = middle + ffn_out
        grad_out = block_cot.astype(jnp.float32)
        inner_grad = jnp.einsum("td,fd->tf", block_cot, w_down, preferred_element_type=jnp.float32)
        gate_grad = (inner_grad * up_value * sigma * (1.0 + gate * (1.0 - sigma))).astype(
            jnp.bfloat16
        )
        up_grad = (inner_grad * active).astype(jnp.bfloat16)
        two_partial = jnp.einsum(
            "tf,df->td", gate_grad, w_gate, preferred_element_type=jnp.float32
        ) + jnp.einsum("tf,df->td", up_grad, w_up, preferred_element_type=jnp.float32)
        normed_two_grad = lax.psum(two_partial, "tensor")
        ffn_gain_grad = jnp.sum(normed_two_grad * plain_two, axis=0)
        middle_grad = grad_out + norm_back(normed_two_grad, plain_two, scale_two, ffn_gain)
        middle_low = middle_grad.astype(jnp.bfloat16)
        mixed_grad = jnp.einsum(
            "td,ed->te", middle_low, w_output, preferred_element_type=jnp.float32
        ).astype(jnp.bfloat16)
        probs_full = jnp.exp(
            jnp.where(allowed[None, None], scores_of(query_rot, key_all), -1e30) - logsum
        )
        probs_low = probs_full.astype(jnp.bfloat16)
        mixed_heads = mixed_grad.reshape(tokens_local, kv_heads, group, HEAD_SIZE)
        prob_grad = jnp.einsum(
            "tkgd,skd->kgts", mixed_heads, value_heads, preferred_element_type=jnp.float32
        )
        value_grad_all = jnp.einsum(
            "kgts,tkgd->skd", probs_low, mixed_heads, preferred_element_type=jnp.float32
        ).reshape(tree_len, kv_width)
        score_grad = (
            probs_full * (prob_grad - jnp.sum(probs_full * prob_grad, axis=-1, keepdims=True))
        ).astype(jnp.bfloat16)
        query_heads = query_rot.reshape(tokens_local, kv_heads, group, HEAD_SIZE)
        key_heads = key_all.reshape(tree_len, kv_heads, HEAD_SIZE)
        query_grad = (
            jnp.einsum(
                "kgts,skd->tkgd", score_grad, key_heads, preferred_element_type=jnp.float32
            ).reshape(tokens_local, q_width)
            * scale
        )
        key_grad_all = (
            jnp.einsum(
                "kgts,tkgd->skd", score_grad, query_heads, preferred_element_type=jnp.float32
            ).reshape(tree_len, kv_width)
            * scale
        )
        key_grad, value_grad = (
            lax.psum_scatter(key_grad_all, "seq", scatter_dimension=0, tiled=True),
            lax.psum_scatter(value_grad_all, "seq", scatter_dimension=0, tiled=True),
        )
        query_low = rotary_back(query_grad, cosine, sine).astype(jnp.bfloat16)
        key_low = rotary_back(key_grad, cosine, sine).astype(jnp.bfloat16)
        value_low = value_grad.astype(jnp.bfloat16)
        one_partial = (
            jnp.einsum("te,de->td", query_low, w_query, preferred_element_type=jnp.float32)
            + jnp.einsum("te,de->td", key_low, key_weight, preferred_element_type=jnp.float32)
            + jnp.einsum("te,de->td", value_low, value_weight, preferred_element_type=jnp.float32)
        )
        normed_one_grad = lax.psum(one_partial.astype(jnp.bfloat16), "tensor").astype(jnp.float32)
        attn_gain_grad = jnp.sum(normed_one_grad * plain_one, axis=0)
        input_grad = middle_grad + norm_back(normed_one_grad, plain_one, scale_one, attn_gain)
        new_grads = (
            grads[0] + outer_sum(normed_one, query_low),
            grads[1] + outer_sum(normed_one, key_low),
            grads[2] + outer_sum(normed_one, value_low),
            grads[3] + outer_sum(mixed, middle_low),
            grads[4] + outer_sum(normed_two, gate_grad),
            grads[5] + outer_sum(normed_two, up_grad),
            grads[6] + outer_sum(inner, block_cot),
        )
        return (
            (new_grads, gain_one + attn_gain_grad, gain_two + ffn_gain_grad),
            (block_out, input_grad),
        )

    zeros = (
        jnp.zeros((width, q_width), jnp.float32),
        jnp.zeros((width, kv_width), jnp.float32),
        jnp.zeros((width, kv_width), jnp.float32),
        jnp.zeros((q_width, width), jnp.float32),
        jnp.zeros((width, ff_width), jnp.float32),
        jnp.zeros((width, ff_width), jnp.float32),
        jnp.zeros((ff_width, width), jnp.float32),
    )
    initial = (zeros, jnp.zeros((width,), jnp.float32), jnp.zeros((width,), jnp.float32))
    carry, (outputs, input_grads) = lax.scan(
        micro, initial, (inputs[0], cotangent[0], segment_ids[0], ancestry[0])
    )
    grads, gain_one, gain_two = carry
    summed = (
        lax.psum_scatter(grads[0], ("dp", "seq"), scatter_dimension=0, tiled=True),
        lax.psum_scatter(grads[1], ("dp", "seq"), scatter_dimension=0, tiled=True),
        lax.psum_scatter(grads[2], ("dp", "seq"), scatter_dimension=0, tiled=True),
        lax.psum_scatter(grads[3], ("dp", "seq"), scatter_dimension=1, tiled=True),
        lax.psum_scatter(grads[4], ("dp", "seq"), scatter_dimension=0, tiled=True),
        lax.psum_scatter(grads[5], ("dp", "seq"), scatter_dimension=0, tiled=True),
        lax.psum_scatter(grads[6], ("dp", "seq"), scatter_dimension=1, tiled=True),
    )
    olds = (mom_query, key_momentum, value_momentum, mom_output, mom_gate, mom_up, mom_down)
    moments = [MU_MUON * olds[index] + summed[index] for index in range(7)]
    standing = [
        moments[0],
        moments[1],
        moments[2],
        moments[3].T,
        moments[4],
        moments[5],
        moments[6].T,
    ]
    squares = [jnp.sum(matrix * matrix) for matrix in standing]
    totals = lax.psum(
        (
            squares[0],
            squares[1],
            squares[2],
            squares[3],
            squares[4],
            squares[5],
            squares[6],
            gain_one,
            gain_two,
        ),
        ("dp", "seq"),
    )
    ortho = [standing[index] / (jnp.sqrt(totals[index]) + EPS_MUON) for index in range(7)]
    for turn in range(ITERS_NS):
        parts = [gram_pieces(matrix) for matrix in ortho]
        grams = (
            lax.psum(parts[0].astype(jnp.bfloat16), ("dp", "seq")).astype(jnp.float32),
            lax.psum(parts[1].astype(jnp.bfloat16), ("dp", "seq")).astype(jnp.float32),
            lax.psum(parts[2].astype(jnp.bfloat16), ("dp", "seq")).astype(jnp.float32),
            lax.psum(parts[3].astype(jnp.bfloat16), ("dp", "seq")).astype(jnp.float32),
            lax.psum(parts[4].astype(jnp.bfloat16), ("dp", "seq")).astype(jnp.float32),
            lax.psum(parts[5].astype(jnp.bfloat16), ("dp", "seq")).astype(jnp.float32),
            lax.psum(parts[6].astype(jnp.bfloat16), ("dp", "seq")).astype(jnp.float32),
        )
        ortho = [newton_step(ortho[index], gram_join(grams[index])) for index in range(7)]
    attn_total = totals[7]
    ffn_total = totals[8]
    factor = -LR_MUON * 0.2 * math.sqrt(MODEL_WIDTH)
    updates = [factor * matrix for matrix in ortho]
    attn_one, attn_two, attn_step = adam(attn_total, attn_first, attn_second)
    ffn_one, ffn_two, ffn_step = adam(ffn_total, ffn_first, ffn_second)
    return (
        outputs[None],
        input_grads[None],
        summed[0],
        summed[1],
        summed[2],
        summed[3],
        summed[4],
        summed[5],
        summed[6],
        attn_total,
        ffn_total,
        moments[0],
        moments[1],
        moments[2],
        moments[3],
        moments[4],
        moments[5],
        moments[6],
        updates[0],
        updates[1],
        updates[2],
        updates[3].T,
        updates[4],
        updates[5],
        updates[6].T,
        attn_one,
        attn_two,
        attn_step,
        ffn_one,
        ffn_two,
        ffn_step,
    )


def solution(mesh):
    placed = (
        P("dp", None, "seq", None),
        P("dp", None, None),
        P("dp", None, None, None),
        P(None, "tensor"),
        P(None, "tensor"),
        P(None, "tensor"),
        P("tensor", None),
        P(None, "tensor"),
        P(None, "tensor"),
        P("tensor", None),
        P(),
        P(),
        P("dp", None, "seq", None),
        P(("dp", "seq"), "tensor"),
        P(("dp", "seq"), "tensor"),
        P(("dp", "seq"), "tensor"),
        P("tensor", ("dp", "seq")),
        P(("dp", "seq"), "tensor"),
        P(("dp", "seq"), "tensor"),
        P("tensor", ("dp", "seq")),
        P(),
        P(),
        P(),
        P(),
    )
    return jax.shard_map(
        shards,
        mesh=mesh,
        in_specs=placed,
        out_specs=(
            P("dp", None, "seq", None),
            P("dp", None, "seq", None),
            P(("dp", "seq"), "tensor"),
            P(("dp", "seq"), "tensor"),
            P(("dp", "seq"), "tensor"),
            P("tensor", ("dp", "seq")),
            P(("dp", "seq"), "tensor"),
            P(("dp", "seq"), "tensor"),
            P("tensor", ("dp", "seq")),
            P(),
            P(),
            P(("dp", "seq"), "tensor"),
            P(("dp", "seq"), "tensor"),
            P(("dp", "seq"), "tensor"),
            P("tensor", ("dp", "seq")),
            P(("dp", "seq"), "tensor"),
            P(("dp", "seq"), "tensor"),
            P("tensor", ("dp", "seq")),
            P(("dp", "seq"), "tensor"),
            P(("dp", "seq"), "tensor"),
            P(("dp", "seq"), "tensor"),
            P("tensor", ("dp", "seq")),
            P(("dp", "seq"), "tensor"),
            P(("dp", "seq"), "tensor"),
            P("tensor", ("dp", "seq")),
            P(),
            P(),
            P(),
            P(),
            P(),
            P(),
        ),
        check_vma=False,
    )
```

profile of v0, /device:TPU:0, one launch (start us, length us, event | category | flops | bytes accessed | tf_op | source)
XLA Modules:
  0.0 2089.3 jit_solution(14900640851728924622)
XLA Ops:
  10.6 976.5 %while.33 = (s32[]{:T(128)}, f32[1536,384]{1,0:T(8,128)}, f32[1536,192]{0,1:T(8,128)}, f32[1536,192]{0,1:T(8,128)}, f32[384,1536]{1,0:T(8,128)}, /*index=5*/f32[...) while((s32[]{:T(128)}, f32[1536,384]{1,0:T(8,128)}, ...), condition=%wide.region_17.18_spmd.clone, body=%wide.region_0.17_spmd.clone.sunk | while | flops 22479355904 | bytes 728028160 | solution.py:293
  16.9 8.8 all_gather.17
  29.7 6.8 all_gather.16
  53.3 5.0 fusion.606
  58.3 115.5 %all-reduce.32.cloned.1.call-done = f32[512,1536]{1,0:T(8,128)} async-done(((f32[512,1536]{1,0:T(8,128)}), f32[512,1536]{1,0:T(8,128)}) %all-reduce.32.cloned.1.call-update) | async-done | bytes 3145744 | tf_op jit(solution)/shard_map/while/body/eval_jaxpr/psum | solution.py:195
  181.6 3.5 multiply_convert_fusion.7
  187.0 3.5 convolution_add_fusion.23
  190.8 119.9 %all-reduce.34.cloned.1.call-done = f32[512,1536]{1,0:T(8,128)} async-done(((f32[512,1536]{1,0:T(8,128)}), f32[512,1536]{1,0:T(8,128)}) %all-reduce.34.cloned.1.call-update) | async-done | bytes 3145744 | tf_op jit(solution)/shard_map/while/body/eval_jaxpr/psum | solution.py:219
  310.7 3.4 multiply_reduce_fusion.13
  327.8 5.2 convolution_convert_fusion.71
  332.9 5.7 fusion.611
  347.0 4.4 convolution_add_fusion.28
  351.4 13.2 reduce-scatter.26.cloned.1.call-done
  364.6 4.0 fusion.613
  368.6 6.4 select_add_fusion.12
  375.1 4.6 select_add_fusion.11
  395.1 94.8 %all-reduce.36.cloned.1.call-done = (bf16[512,1536]{1,0:T(8,128)(2,1)}, bf16[512,1536]{1,0:T(8,128)(2,1)}) async-done(((bf16[512,1536]{1,0:T(8,128)(2,1)}, bf16[512,1536]{1,0:T(8,128)(2,1)}), (bf16[512,1536]{1,0:T(8,128)(2,1)}, bf16[512,1536]{1,0:T(8,128)(2,1)})) %all-reduce.36.cloned.1.call-update) | async-done | bytes 3145744 | tf_op jit(solution)/shard_map/while/body/eval_jaxpr/psum | solution.py:266
  493.0 6.0 fusion.615
  505.0 7.4 all_gather.17
  516.3 6.4 all_gather.16
  539.5 5.0 fusion.606
  544.5 113.8 %all-reduce.32.cloned.1.call-done = f32[512,1536]{1,0:T(8,128)} async-done(((f32[512,1536]{1,0:T(8,128)}), f32[512,1536]{1,0:T(8,128)}) %all-reduce.32.cloned.1.call-update) | async-done | bytes 3145744 | tf_op jit(solution)/shard_map/while/body/eval_jaxpr/psum | solution.py:195
  666.2 3.5 multiply_convert_fusion.7
  671.6 3.5 convolution_add_fusion.23
  675.5 119.7 %all-reduce.34.cloned.1.call-done = f32[512,1536]{1,0:T(8,128)} async-done(((f32[512,1536]{1,0:T(8,128)}), f32[512,1536]{1,0:T(8,128)}) %all-reduce.34.cloned.1.call-update) | async-done | bytes 3145744 | tf_op jit(solution)/shard_map/while/body/eval_jaxpr/psum | solution.py:219
  795.3 3.4 multiply_reduce_fusion.13
  812.3 5.2 convolution_convert_fusion.71
  817.5 5.7 fusion.611
  831.5 4.4 convolution_add_fusion.28
  835.9 13.5 reduce-scatter.26.cloned.1.call-done
  849.3 4.0 fusion.613
  853.3 8.2 select_add_fusion.12
  861.5 7.5 select_add_fusion.11
  885.4 89.1 %all-reduce.36.cloned.1.call-done = (bf16[512,1536]{1,0:T(8,128)(2,1)}, bf16[512,1536]{1,0:T(8,128)(2,1)}) async-done(((bf16[512,1536]{1,0:T(8,128)(2,1)}, bf16[512,1536]{1,0:T(8,128)(2,1)}), (bf16[512,1536]{1,0:T(8,128)(2,1)}, bf16[512,1536]{1,0:T(8,128)(2,1)})) %all-reduce.36.cloned.1.call-update) | async-done | bytes 3145744 | tf_op jit(solution)/shard_map/while/body/eval_jaxpr/psum | solution.py:266
  977.7 6.0 fusion.615
  997.4 6.8 copy.65
  1004.3 24.4 %reduce-scatter.12.cloned.1.call-done = f32[192,192]{1,0:T(8,128)} async-done(((f32[1536,192]{1,0:T(8,128)}), f32[192,192]{1,0:T(8,128)}) %reduce-scatter.12.cloned.1.call-update) | async-done | bytes 147472 | tf_op jit(solution)/shard_map/reduce_scatter | solution.py:299
  1031.0 39.8 %reduce-scatter.14.cloned.1.call-done = f32[192,192]{1,0:T(8,128)} async-done(((f32[1536,192]{1,0:T(8,128)}), f32[192,192]{1,0:T(8,128)}) %reduce-scatter.14.cloned.1.call-update) | async-done | bytes 147472 | tf_op jit(solution)/shard_map/reduce_scatter | solution.py:300
  1073.0 43.8 %reduce-scatter.10.cloned.1.call-done = f32[192,384]{1,0:T(8,128)} async-done(((f32[1536,384]{1,0:T(8,128)}), f32[192,384]{1,0:T(8,128)}) %reduce-scatter.10.cloned.1.call-update) | async-done | bytes 294928 | tf_op jit(solution)/shard_map/reduce_scatter | solution.py:298
  1118.5 44.6 %reduce-scatter.16.cloned.1.call-done = f32[384,192]{0,1:T(8,128)} async-done(((f32[384,1536]{0,1:T(8,128)}), f32[384,192]{0,1:T(8,128)}) %reduce-scatter.16.cloned.1.call-update) | async-done | bytes 294928 | tf_op jit(solution)/shard_map/reduce_scatter | solution.py:301
  1164.7 63.9 %reduce-scatter.20.cloned.1.call-done = f32[192,1024]{1,0:T(8,128)} async-done(((f32[1536,1024]{1,0:T(8,128)}), f32[192,1024]{1,0:T(8,128)}) %reduce-scatter.20.cloned.1.call-update) | async-done | bytes 786448 | tf_op jit(solution)/shard_map/reduce_scatter | solution.py:303
  1230.6 63.6 %reduce-scatter.18.cloned.1.call-done = f32[192,1024]{1,0:T(8,128)} async-done(((f32[1536,1024]{1,0:T(8,128)}), f32[192,1024]{1,0:T(8,128)}) %reduce-scatter.18.cloned.1.call-update) | async-done | bytes 786448 | tf_op jit(solution)/shard_map/reduce_scatter | solution.py:302
  1296.2 63.5 %reduce-scatter.22.cloned.1.call-done = f32[1024,192]{0,1:T(8,128)} async-done(((f32[1024,1536]{0,1:T(8,128)}), f32[1024,192]{0,1:T(8,128)}) %reduce-scatter.22.cloned.1.call-update) | async-done | bytes 786448 | tf_op jit(solution)/shard_map/reduce_scatter | solution.py:304
  1361.9 25.1 %all-reduce.1 = (f32[1536]{0:T(1024)S(1)}, f32[1536]{0:T(1024)S(1)}, f32[]{:T(128)}, f32[]{:T(128)}, f32[]{:T(128)}, /*index=5*/f32[]{:T(128)}, f32[]{:T(128)}, f32[]{:T(128)}, f32[]{:T(128)}) all-reduce(f32[1536]{0:T(1024)S(1)} %copy-done.162, f32[1536]{0:T(1024)S(1)} %copy-done.159, ...), channel_id=1, replica_groups=mesh['dp'=4,'seq'=2,'tensor'=4] {'dp','seq'}, use_global_device_ids=true, to_apply=%region_25.26 | all-reduce | flops 3079 | bytes 24632 | tf_op jit(solution)/shard_map/psum | solution.py:318
  1431.8 45.2 %all-reduce.24.cloned.1.call-done = (bf16[3,96,96]{2,1,0:T(8,128)(2,1)}, bf16[3,96,96]{2,1,0:T(8,128)(2,1)}) async-done(((bf16[3,96,96]{2,1,0:T(8,128)(2,1)}, bf16[3,96,96]{2,1,0:T(8,128)(2,1)}), (bf16[3,96,96]{2,1,0:T(8,128)(2,1)}, bf16[3,96,96]{2,1,0:T(8,128)(2,1)})) %all-reduce.24.cloned.1.call-update) | async-done | bytes 110608 | tf_op jit(solution)/shard_map/psum | solution.py:337
  1484.6 90.7 %all-reduce.30.cloned.1.call-done = (bf16[3,192,192]{2,1,0:T(8,128)(2,1)}, bf16[3,192,192]{2,1,0:T(8,128)(2,1)}, bf16[3,512,512]{2,1,0:T(8,128)(2,1)}, bf16[3,512,512]{2,1,0:T(8,128)(2,1)}, bf16[3,512,512]{2,1,0:T(8,128)(2,1)}) async-done(((bf16[3,192,192]{2,1,0:T(8,128)(2,1)}, bf16[3,192,192]{2,1,0:T(8,128)(2,1)}, bf16[3,512,512]{2,1,0:T(8,128)(2,1)}, bf16[3,512,512]{2,1,0:T(8,128)(2,1)}, ...) | async-done | bytes 5160976 | tf_op jit(solution)/shard_map/psum | solution.py:336
  1592.3 19.6 fusion.109
  1612.0 4.3 multiply_add_fusion.4
  1625.6 19.8 fusion.112
  1645.5 3.4 fusion.146
  1657.4 19.8 fusion.115
  1697.6 85.6 %all-reduce.28.cloned.1.call-done = (bf16[3,192,192]{2,1,0:T(8,128)(2,1)}, bf16[3,192,192]{2,1,0:T(8,128)(2,1)}, bf16[3,512,512]{2,1,0:T(8,128)(2,1)}, bf16[3,512,512]{2,1,0:T(8,128)(2,1)}, bf16[3,512,512]{2,1,0:T(8,128)(2,1)}) async-done(((bf16[3,192,192]{2,1,0:T(8,128)(2,1)}, bf16[3,192,192]{2,1,0:T(8,128)(2,1)}, bf16[3,512,512]{2,1,0:T(8,128)(2,1)}, bf16[3,512,512]{2,1,0:T(8,128)(2,1)}, ...) | async-done | bytes 5160976 | tf_op jit(solution)/shard_map/psum | solution.py:336
  1806.5 19.9 fusion.108
  1826.5 4.2 multiply_add_fusion.3
  1840.1 19.8 fusion.111
  1860.0 3.4 fusion.149
  1872.7 19.5 fusion.114
  1910.5 87.8 %all-reduce.26.cloned.1.call-done = (bf16[3,192,192]{2,1,0:T(8,128)(2,1)}, bf16[3,192,192]{2,1,0:T(8,128)(2,1)}, bf16[3,512,512]{2,1,0:T(8,128)(2,1)}, bf16[3,512,512]{2,1,0:T(8,128)(2,1)}, bf16[3,512,512]{2,1,0:T(8,128)(2,1)}) async-done(((bf16[3,192,192]{2,1,0:T(8,128)(2,1)}, bf16[3,192,192]{2,1,0:T(8,128)(2,1)}, bf16[3,512,512]{2,1,0:T(8,128)(2,1)}, bf16[3,512,512]{2,1,0:T(8,128)(2,1)}, ...) | async-done | bytes 5160976 | tf_op jit(solution)/shard_map/psum | solution.py:336
  2017.7 19.1 fusion.110
  2036.9 4.2 fusion.155
  2041.2 14.3 fusion.113
  2055.6 4.2 fusion.143
  2062.8 14.1 fusion.107
  2076.9 4.6 fusion.161
  (826 shorter events, 364.5 us)
Async XLA Ops:
  11.1 162.7 %all-reduce.32.cloned.1.call-start = ((), (), s32[]{:S(2)}) async-start(), calls=%async_computation.22 | async-start | bytes 6291456 | tf_op jit(solution)/shard_map/while/body/eval_jaxpr/psum | solution.py:195
  12.9 25.9 %copy-start.87 = (f32[512]{0:T(512)}, f32[512]{0:T(512)S(1)}, u32[]{:S(2)}) copy-start(f32[512]{0:T(512)S(1)} %add_rsqrt_fusion.4) | copy-start | bytes 6148 | tf_op jit(solution)/shard_map/while
  51.4 259.3 %all-reduce.34.cloned.1.call-start = ((), (), s32[]{:S(2)}) async-start(), calls=%async_computation.23 | async-start | bytes 6291456 | tf_op jit(solution)/shard_map/while/body/eval_jaxpr/psum | solution.py:219
  58.3 118.4 %copy-start.86 = (f32[1536]{0:T(1024)S(1)}, f32[1536]{0:T(1024)}, u32[]{:S(2)}) copy-start(f32[1536]{0:T(1024)} %get-tuple-element.1063) | copy-start | bytes 18436 | tf_op jit(solution)/shard_map/while
  190.5 154.6 %reduce-scatter.24.cloned.1.call-start = ((), (), s32[]{:S(2)}) async-start(), calls=%async_computation.24 | async-start | bytes 1179648 | tf_op jit(solution)/shard_map/while/body/eval_jaxpr/reduce_scatter | solution.py:255
  327.7 36.9 %reduce-scatter.26.cloned.1.call-start = ((), (), s32[]{:S(2)}) async-start(), calls=%async_computation.25 | async-start | bytes 1179648 | tf_op jit(solution)/shard_map/while/body/eval_jaxpr/reduce_scatter | solution.py:256
  338.7 151.2 %all-reduce.36.cloned.1.call-start = ((), (), s32[]{:S(2)}) async-start(), calls=%async_computation.26 | async-start | bytes 6291456 | tf_op jit(solution)/shard_map/while/body/eval_jaxpr/psum | solution.py:266
  393.3 99.7 %copy-start.160 = (f32[1536]{0:T(1024)S(1)}, f32[1536]{0:T(1024)}, u32[]{:S(2)}) copy-start(f32[1536]{0:T(1024)} %get-tuple-element.1019) | copy-start | bytes 18436 | tf_op jit(solution)/shard_map/while
  499.1 159.2 %all-reduce.32.cloned.1.call-start = ((), (), s32[]{:S(2)}) async-start(), calls=%async_computation.22 | async-start | bytes 6291456 | tf_op jit(solution)/shard_map/while/body/eval_jaxpr/psum | solution.py:195
  501.0 24.1 %copy-start.87 = (f32[512]{0:T(512)}, f32[512]{0:T(512)S(1)}, u32[]{:S(2)}) copy-start(f32[512]{0:T(512)S(1)} %add_rsqrt_fusion.4) | copy-start | bytes 6148 | tf_op jit(solution)/shard_map/while
  537.6 257.6 %all-reduce.34.cloned.1.call-start = ((), (), s32[]{:S(2)}) async-start(), calls=%async_computation.23 | async-start | bytes 6291456 | tf_op jit(solution)/shard_map/while/body/eval_jaxpr/psum | solution.py:219
  544.5 116.7 %copy-start.86 = (f32[1536]{0:T(1024)S(1)}, f32[1536]{0:T(1024)}, u32[]{:S(2)}) copy-start(f32[1536]{0:T(1024)} %get-tuple-element.1063) | copy-start | bytes 18436 | tf_op jit(solution)/shard_map/while
  675.1 154.5 %reduce-scatter.24.cloned.1.call-start = ((), (), s32[]{:S(2)}) async-start(), calls=%async_computation.24 | async-start | bytes 1179648 | tf_op jit(solution)/shard_map/while/body/eval_jaxpr/reduce_scatter | solution.py:255
  812.3 37.1 %reduce-scatter.26.cloned.1.call-start = ((), (), s32[]{:S(2)}) async-start(), calls=%async_computation.25 | async-start | bytes 1179648 | tf_op jit(solution)/shard_map/while/body/eval_jaxpr/reduce_scatter | solution.py:256
  823.2 151.3 %all-reduce.36.cloned.1.call-start = ((), (), s32[]{:S(2)}) async-start(), calls=%async_computation.26 | async-start | bytes 6291456 | tf_op jit(solution)/shard_map/while/body/eval_jaxpr/psum | solution.py:266
  882.3 95.3 %copy-start.160 = (f32[1536]{0:T(1024)S(1)}, f32[1536]{0:T(1024)}, u32[]{:S(2)}) copy-start(f32[1536]{0:T(1024)} %get-tuple-element.1019) | copy-start | bytes 18436 | tf_op jit(solution)/shard_map/while
  987.1 41.6 %reduce-scatter.12.cloned.1.call-start = ((), (), s32[]{:S(2)}) async-start(), calls=%async_computation.10 | async-start | bytes 1769472 | tf_op jit(solution)/shard_map/reduce_scatter | solution.py:299
  990.1 80.7 %reduce-scatter.14.cloned.1.call-start = ((), (), s32[]{:S(2)}) async-start(), calls=%async_computation.11 | async-start | bytes 1769472 | tf_op jit(solution)/shard_map/reduce_scatter | solution.py:300
  993.2 123.6 %reduce-scatter.10.cloned.1.call-start = ((), (), s32[]{:S(2)}) async-start(), calls=%async_computation.9 | async-start | bytes 2654208 | tf_op jit(solution)/shard_map/reduce_scatter | solution.py:298
  993.8 169.2 %reduce-scatter.16.cloned.1.call-start = ((), (), s32[]{:S(2)}) async-start(), calls=%async_computation.12 | async-start | bytes 2654208 | tf_op jit(solution)/shard_map/reduce_scatter | solution.py:301
  995.8 232.8 %reduce-scatter.20.cloned.1.call-start = ((), (), s32[]{:S(2)}) async-start(), calls=%async_computation.14 | async-start | bytes 7077888 | tf_op jit(solution)/shard_map/reduce_scatter | solution.py:303
  996.6 297.6 %reduce-scatter.18.cloned.1.call-start = ((), (), s32[]{:S(2)}) async-start(), calls=%async_computation.13 | async-start | bytes 7077888 | tf_op jit(solution)/shard_map/reduce_scatter | solution.py:302
  997.3 362.3 %reduce-scatter.22.cloned.1.call-start = ((), (), s32[]{:S(2)}) async-start(), calls=%async_computation.15 | async-start | bytes 7077888 | tf_op jit(solution)/shard_map/reduce_scatter | solution.py:304
  1004.2 24.5 %copy-start.163 = (f32[192,192]{1,0:T(8,128)S(1)}, f32[192,192]{1,0:T(8,128)}, u32[]{:S(2)}) copy-start(f32[192,192]{1,0:T(8,128)} %param.40) | copy-start | bytes 442372
  1004.2 66.5 %copy-start.164 = (f32[192,192]{1,0:T(8,128)S(1)}, f32[192,192]{1,0:T(8,128)}, u32[]{:S(2)}) copy-start(f32[192,192]{1,0:T(8,128)} %param.41) | copy-start | bytes 442372
  1004.2 112.6 %copy-start.152 = (f32[192,384]{1,0:T(8,128)S(1)}, f32[192,384]{1,0:T(8,128)}, u32[]{:S(2)}) copy-start(f32[192,384]{1,0:T(8,128)} %param.39) | copy-start | bytes 884740
  1004.2 158.8 %copy-start.153 = (f32[384,192]{0,1:T(8,128)S(1)}, f32[384,192]{0,1:T(8,128)}, u32[]{:S(2)}) copy-start(f32[384,192]{0,1:T(8,128)} %param.42) | copy-start | bytes 884740
  1004.2 224.4 %copy-start.133 = (f32[192,1024]{1,0:T(8,128)S(1)}, f32[192,1024]{1,0:T(8,128)}, u32[]{:S(2)}) copy-start(f32[192,1024]{1,0:T(8,128)} %param.44) | copy-start | bytes 2359300
  1004.3 290.0 %copy-start.134 = (f32[192,1024]{1,0:T(8,128)S(1)}, f32[192,1024]{1,0:T(8,128)}, u32[]{:S(2)}) copy-start(f32[192,1024]{1,0:T(8,128)} %param.43) | copy-start | bytes 2359300
  1004.3 472.8 %all-reduce.24.cloned.1.call-start = ((), (), s32[]{:S(2)}) async-start(), calls=%async_computation.18 | async-start | bytes 294912 | tf_op jit(solution)/shard_map/psum | solution.py:337
  1118.4 277.8 %copy-start.95 = (f32[192,384]{1,0:T(8,128)}, f32[192,384]{1,0:T(8,128)S(1)}, u32[]{:S(2)}) copy-start(f32[192,384]{1,0:T(8,128)S(1)} %get-tuple-element.638) | copy-start | bytes 884740
  1164.7 235.5 %copy-start.66 = (f32[384,192]{0,1:T(8,128)}, f32[384,192]{0,1:T(8,128)S(1)}, u32[]{:S(2)}) copy-start(f32[384,192]{0,1:T(8,128)S(1)} %get-tuple-element.632) | copy-start | bytes 884740
  1164.7 197.2 %copy-start.159 = (f32[1536]{0:T(1024)S(1)}, f32[1536]{0:T(1024)}, u32[]{:S(2)}) copy-start(f32[1536]{0:T(1024)} %get-tuple-element.408) | copy-start | bytes 18436
  1164.7 197.2 %copy-start.162 = (f32[1536]{0:T(1024)S(1)}, f32[1536]{0:T(1024)}, u32[]{:S(2)}) copy-start(f32[1536]{0:T(1024)} %get-tuple-element.407) | copy-start | bytes 18436
  1230.6 180.6 %copy-start.43 = (f32[192,1024]{1,0:T(8,128)}, f32[192,1024]{1,0:T(8,128)S(1)}, u32[]{:S(2)}) copy-start(f32[192,1024]{1,0:T(8,128)S(1)} %get-tuple-element.628) | copy-start | bytes 2359300
  1230.6 161.9 %copy-start.135 = (f32[192,192]{1,0:T(8,128)S(1)}, f32[192,192]{1,0:T(8,128)}, u32[]{:S(2)}) copy-start(f32[192,192]{1,0:T(8,128)} %get-tuple-element.634) | copy-start | bytes 442372
  1296.2 108.5 %copy-start.44 = (f32[192,1024]{1,0:T(8,128)}, f32[192,1024]{1,0:T(8,128)S(1)}, u32[]{:S(2)}) copy-start(f32[192,1024]{1,0:T(8,128)S(1)} %get-tuple-element.630) | copy-start | bytes 2359300
  1361.9 55.9 %copy-start.45 = (f32[1024,192]{0,1:T(8,128)}, f32[1024,192]{0,1:T(8,128)S(1)}, u32[]{:S(2)}) copy-start(f32[1024,192]{0,1:T(8,128)S(1)} %get-tuple-element.626) | copy-start | bytes 2359300
  1387.0 517.9 %copy-start.169 = (f32[1536]{0:T(1024)}, f32[1536]{0:T(1024)S(1)}, u32[]{:S(2)}) copy-start(f32[1536]{0:T(1024)S(1)} %get-tuple-element.587) | copy-start | bytes 18436
  1387.0 517.9 %copy-start.170 = (f32[1536]{0:T(1024)}, f32[1536]{0:T(1024)S(1)}, u32[]{:S(2)}) copy-start(f32[1536]{0:T(1024)S(1)} %get-tuple-element.588) | copy-start | bytes 18436
  1425.6 149.8 %all-reduce.30.cloned.1.call-start = ((), (), s32[]{:S(2)}) async-start(), calls=%async_computation.21 | async-start | bytes 10616832 | tf_op jit(solution)/shard_map/psum | solution.py:336
  1431.7 47.8 %copy-start.59 = (f32[192,192]{1,0:T(8,128)S(1)}, f32[192,192]{1,0:T(8,128)}, u32[]{:S(2)}) copy-start(f32[192,192]{1,0:T(8,128)} %copy-done.58) | copy-start | bytes 442372
  1431.7 50.5 %copy-start.57 = (f32[192,192]{1,0:T(8,128)S(1)}, f32[192,192]{1,0:T(8,128)}, u32[]{:S(2)}) copy-start(f32[192,192]{1,0:T(8,128)} %copy-done.56) | copy-start | bytes 442372
  1431.8 258.3 %all-reduce.22.cloned.1.call-start = ((), (), s32[]{:S(2)}) async-start(), calls=%async_computation.17 | async-start | bytes 294912 | tf_op jit(solution)/shard_map/psum | solution.py:337
  1484.6 298.6 %all-reduce.28.cloned.1.call-start = ((), (), s32[]{:S(2)}) async-start(), calls=%async_computation.20 | async-start | bytes 10616832 | tf_op jit(solution)/shard_map/psum | solution.py:336
  1625.6 19.9 copy-start.111
  1625.6 19.9 copy-start.112
  1625.6 19.9 copy-start.113
  1625.6 19.9 copy-start.128
  1657.4 19.8 copy-start.116
  1657.4 19.8 copy-start.129
  1689.8 215.8 %all-reduce.20.cloned.1.call-start = ((), (), s32[]{:S(2)}) async-start(), calls=%async_computation.16 | async-start | bytes 294912 | tf_op jit(solution)/shard_map/psum | solution.py:337
  1695.6 93.4 %copy-start.60 = (f32[192,192]{1,0:T(8,128)}, f32[192,192]{1,0:T(8,128)S(1)}, u32[]{:S(2)}) copy-start(f32[192,192]{1,0:T(8,128)S(1)} %convolution_add_fusion.12) | copy-start | bytes 442372
  1697.6 300.7 %all-reduce.26.cloned.1.call-start = ((), (), s32[]{:S(2)}) async-start(), calls=%async_computation.19 | async-start | bytes 10616832 | tf_op jit(solution)/shard_map/psum | solution.py:336
  1806.4 20.0 copy-start.49
  1806.4 20.0 copy-start.108
  1806.4 20.0 copy-start.109
  1806.4 20.0 copy-start.110
  1806.5 20.0 copy-start.127
  1840.1 19.8 copy-start.51
  1840.1 19.8 copy-start.117
  1840.1 19.9 copy-start.118
  1840.1 19.9 copy-start.119
  1840.1 19.9 copy-start.130
  (196 other events, 1079.4 us)
Sparse Core Ops, SparseCore 0:
  51.5 122.2 all-reduce.31
  190.6 120.0 all-reduce.33
  327.9 16.5 reduce-scatter.23
  347.1 17.4 reduce-scatter.25
  368.7 121.0 all-reduce.35
  537.8 120.5 all-reduce.31
  675.2 120.0 all-reduce.33
  812.4 16.5 reduce-scatter.23
  831.8 17.4 reduce-scatter.25
  853.4 121.0 all-reduce.35
Sparse Core Ops, SparseCore 1:
  991.5 37.2 reduce-scatter.11
  1032.5 38.2 reduce-scatter.13
  1074.5 42.2 reduce-scatter.9
  1120.7 42.2 reduce-scatter.15
  1167.0 61.6 reduce-scatter.19
  1232.6 61.6 reduce-scatter.17
  1298.0 61.6 reduce-scatter.21
  1425.7 51.3 all-reduce.23
  1481.4 93.9 all-reduce.29
  1578.6 52.1 all-reduce.21
  1689.8 93.3 all-reduce.27
  1786.4 52.1 all-reduce.19
  1904.9 93.3 all-reduce.25
where the time goes:
time: 2100 us; the launch traced here: 2090 us
  waiting for transfers between devices  1330 us (63%)
  matrix products  469 us (22%)
  other arithmetic  104 us (5%)
  local copies, waits for them, and re-layouts  96 us (5%)
  blocking collectives  54.6 us (3%)
  between operations  23 us (1%)
    psum x3, waiting for transfers between devices, shards(): lax.psum(parts[0].astype(jnp.bfloat16), ('dp', 'seq')).astype(jnp.float32)  264 us
    psum x2, waiting for transfers between devices, micro(): normed_two_grad = lax.psum(two_partial, 'tensor')  240 us
    psum x2, waiting for transfers between devices, micro(): lax.psum(jnp.dot(mixed, w_output, preferred_element_type=jnp.float32), 't...  229 us
    psum x2, waiting for transfers between devices, micro(): lax.psum(one_partial.astype(jnp.bfloat16), 'tensor').astype(jnp.float32)  184 us
    dot_general x21, matrix products, newton_step(): poly = NS_B * gram + NS_C * jnp.dot(gram, gram, precision=HIGH)  180 us
    reduce_scatter x1, waiting for transfers between devices, shards(): lax.psum_scatter(grads[5], ('dp', 'seq'), scatter_dimension=0, tiled=True)  63.9 us
    reduce_scatter x1, waiting for transfers between devices, shards(): lax.psum_scatter(grads[4], ('dp', 'seq'), scatter_dimension=0, tiled=True)  63.6 us
    reduce_scatter x1, waiting for transfers between devices, shards(): lax.psum_scatter(grads[6], ('dp', 'seq'), scatter_dimension=1, tiled=True)  63.5 us
  transfers between devices with their start and end apart: 23, of which 19 were waited for; matrix products, arithmetic and copies ran while one was open for 18% of the time, Pallas kernels for 0%

commit v1 on v0

v1 whole, which is shorter than its diff:
```python
import functools
import math

import jax
import jax.numpy as jnp
from jax import lax
from jax.experimental import pallas as pl
from jax.experimental.pallas import tpu as pltpu
from jax.sharding import PartitionSpec as P

MODEL_WIDTH = 1536
HEAD_SIZE = 96
ITERS_NS = 3
ADAM_STEP = 10


EPS_NORM = 1e-05
ROPE_THETA = 100000.0
MU_MUON = 0.95
NS_A = 3.4445
NS_B = -4.775
NS_C = 2.0315
LR_MUON = 0.1
EPS_MUON = 1e-07
BETA_ONE = 0.9
BETA_TWO = 0.95
LR_ADAM = 0.01
EPS_ADAM = 1e-08
LOW = jnp.bfloat16
F32 = jnp.float32


def rms_scale(values):
    return lax.rsqrt(jnp.mean(values * values, axis=-1, keepdims=True) + EPS_NORM)


def norm_back(upstream, plain, scale, gain):
    scaled = upstream * gain
    return scale * (scaled - plain * jnp.mean(scaled * plain, axis=-1, keepdims=True))


def rotary_tables(positions):
    half = HEAD_SIZE // 2
    freq = jnp.power(ROPE_THETA, -(2.0 * jnp.arange(half, dtype=F32)) / HEAD_SIZE)
    angle = positions[..., None] * freq
    return (jnp.cos(angle), jnp.sin(angle))


def rotary(values, cosine, sine):
    shape = values.shape
    heads = values.reshape(shape[:-1] + (shape[-1] // HEAD_SIZE, HEAD_SIZE))
    half = HEAD_SIZE // 2
    front = heads[..., :half]
    back = heads[..., half:]
    cos_h = cosine[..., None, :]
    sin_h = sine[..., None, :]
    return jnp.concatenate(
        [front * cos_h - back * sin_h, back * cos_h + front * sin_h], axis=-1
    ).reshape(shape)


def dot(left, right):
    return jnp.dot(left, right, preferred_element_type=F32)


def dot_nt(left, right):
    return lax.dot_general(left, right, (((1,), (1,)), ((), ())), preferred_element_type=F32)


def dot_tn(left, right):
    return lax.dot_general(left, right, (((0,), (0,)), ((), ())), preferred_element_type=F32)


def owner_bits(seq_size, dp_size):
    return (seq_size.bit_length() - 1, seq_size.bit_length() + dp_size.bit_length() - 2)


def my_bit(bit, seq_bits):
    if bit < seq_bits:
        return (lax.axis_index("seq") // 2**bit) % 2
    return (lax.axis_index("dp") // 2 ** (bit - seq_bits)) % 2


def partner_of(bit, seq_bits):
    axis, power = ("seq", 2**bit) if bit < seq_bits else ("dp", 2 ** (bit - seq_bits))
    return {axis: lax.axis_index(axis) + power * (1 - 2 * my_bit(bit, seq_bits))}


def exchange_kernel(count, bits, seq_bits, chunks, gather, *refs):
    sources, outs, refs = refs[:count], refs[count : 2 * count], refs[2 * count :]
    held = [refs[stage * count : (stage + 1) * count] for stage in range(bits)]
    refs = refs[bits * count :]
    if gather:
        whole, refs = refs[:count], refs[count:]
    send_sem, recv_sem, out_sem = refs
    every = list(range(bits - 1, -1, -1))
    core = min(seq_bits, bits - 1)
    rest = [bit for bit in every if bit != core]
    me = {bit: my_bit(bit, seq_bits) for bit in every}
    there = {bit: partner_of(bit, seq_bits) for bit in every}
    copies = []

    barrier = pltpu.get_barrier_semaphore()
    for bit in every:
        pl.semaphore_signal(
            barrier, inc=1, device_id=there[bit], device_id_type=pl.DeviceIdType.MESH
        )
    pl.semaphore_wait(barrier, bits)

    def order_of(number):
        turn = number % len(rest)
        return [core] + rest[turn:] + rest[:turn]

    def place(left, chosen, columns):
        return tuple(chosen.get(bit, slice(None)) for bit in left) + (slice(None), columns)

    def send(source, target, slot, number, bit):
        copy = pltpu.make_async_remote_copy(
            src_ref=source,
            dst_ref=target,
            send_sem=send_sem.at[slot, number],
            recv_sem=recv_sem.at[slot, number],
            device_id=there[bit],
            device_id_type=pl.DeviceIdType.MESH,
        )
        copy.start()
        copies.append(copy)
        return copy

    arriving = {}
    for number, (index, columns) in enumerate(chunks):
        left = list(every)
        source = sources[index].at[place(left, {core: 1 - me[core]}, columns)]
        left.remove(core)
        target = held[0][index].at[place(left, {}, columns)]
        arriving[number] = send(source, target, 0, number, core)

    def summed(number, stage, chosen):
        index, columns = chunks[number]
        order = order_of(number)
        known = dict(chosen)
        for bit in order[:stage]:
            known[bit] = me[bit]
        left = list(every)
        total = sources[index][place(left, known, columns)].astype(F32)
        for past in range(stage):
            left = [bit for bit in left if bit != order[past]]
            total = total + held[past][index][place(left, known, columns)].astype(F32)
        return total

    for stage in range(1, bits):
        for number, (index, columns) in enumerate(chunks):
            order = order_of(number)
            bit = order[stage]
            arriving[number].wait_recv()
            left = [b for b in every if b not in order[:stage]]
            spot = place(left, {bit: 1 - me[bit]}, columns)
            held[stage - 1][index][spot] = summed(number, stage, {bit: 1 - me[bit]}).astype(LOW)
            left.remove(bit)
            target = held[stage][index].at[place(left, {}, columns)]
            arriving[number] = send(held[stage - 1][index].at[spot], target, stage, number, bit)

    for number, (index, columns) in enumerate(chunks):
        arriving[number].wait_recv()
        total = summed(number, bits, {})
        if not gather:
            outs[index][:, columns] = total
            continue
        order = order_of(number)
        spot = place(every, me, columns)
        whole[index][spot] = total.astype(LOW)
        target = whole[index].at[spot]
        arriving[number] = send(target, target, bits, number, order[-1])

    if gather:
        for back in range(1, bits):
            for number, (index, columns) in enumerate(chunks):
                order = order_of(number)
                arriving[number].wait_recv()
                known = {bit: me[bit] for bit in order[: bits - back]}
                target = whole[index].at[place(every, known, columns)]
                arriving[number] = send(target, target, bits + back, number, order[bits - back - 1])
        for number in range(len(chunks)):
            arriving[number].wait_recv()
        for copy in copies:
            copy.wait_send()
        locals_ = [
            pltpu.make_async_copy(whole[index], outs[index], out_sem.at[index])
            for index in range(count)
        ]
        for copy in locals_:
            copy.start()
        for copy in locals_:
            copy.wait()
    else:
        for copy in copies:
            copy.wait_send()


def exchange(arrays, sizes, name, number, gather=False, chunk=512):
    seq_bits, bits = owner_bits(*sizes)
    parts = 2**bits
    views, chunks = [], []
    for index, array in enumerate(arrays):
        rows, columns = array.shape
        views.append(array.reshape((2,) * bits + (rows // parts, columns)))
        step = chunk if columns % chunk == 0 else columns
        for begin in range(0, columns, step):
            chunks.append((index, pl.ds(begin, step)))
    count = len(arrays)
    shapes = [view.shape[bits:] for view in views]
    scratch = [
        pltpu.VMEM((2,) * (bits - 1 - stage) + shape, LOW) for stage in range(bits) for shape in shapes
    ]
    slots = bits
    if gather:
        scratch += [pltpu.VMEM((2,) * bits + shape, LOW) for shape in shapes]
        slots = 2 * bits
        out_shape = [jax.ShapeDtypeStruct((2,) * bits + shape, LOW) for shape in shapes]
        out_specs = [pl.BlockSpec(memory_space=pl.ANY)] * count
    else:
        out_shape = [jax.ShapeDtypeStruct(shape, F32) for shape in shapes]
        out_specs = [pl.BlockSpec(memory_space=pltpu.VMEM)] * count
    scratch += [
        pltpu.SemaphoreType.DMA((slots, len(chunks))),
        pltpu.SemaphoreType.DMA((slots, len(chunks))),
        pltpu.SemaphoreType.DMA((count,)),
    ]
    moved = sum(view.size for view in views) * 2
    results = pl.pallas_call(
        functools.partial(exchange_kernel, count, bits, seq_bits, chunks, gather),
        out_shape=out_shape,
        in_specs=[pl.BlockSpec(memory_space=pltpu.VMEM)] * count,
        out_specs=out_specs,
        scratch_shapes=scratch,
        compiler_params=pltpu.CompilerParams(
            collective_id=number, has_side_effects=True, vmem_limit_bytes=48 * 2**20
        ),
        cost_estimate=pl.CostEstimate(flops=0, bytes_accessed=16 * moved, transcendentals=0),
        name=name,
    )(*views)
    if gather:
        results = [r.reshape(a.shape) for r, a in zip(results, arrays)]
    return results


def schulz_kernel(packed, tile, gram_ref, moment_ref, step_ref, gram, low_gram, poly, low_poly, low_mix):
    size = gram.shape[0]
    tiles = size // tile

    def rows(step):
        return pl.ds(pl.multiple_of(step * tile, tile), tile)

    if packed:
        half = size // 2
        gram[:half, :half] = gram_ref[0].astype(F32)
        gram[:half, half:] = gram_ref[1].astype(F32)
        gram[half:, :half] = gram_ref[1].astype(F32).T
        gram[half:, half:] = gram_ref[2].astype(F32)
    else:
        gram[...] = gram_ref[...].astype(F32)

    def diagonal(step, total):
        block = gram[rows(step), :]
        row = lax.broadcasted_iota(jnp.int32, block.shape, 0) + step * tile
        column = lax.broadcasted_iota(jnp.int32, block.shape, 1)
        return total + jnp.sum(
            jnp.sum(jnp.where(row == column, block, 0.0), axis=0, keepdims=True),
            axis=1,
            keepdims=True,
        )

    trace = lax.fori_loop(0, tiles, diagonal, jnp.zeros((1, 1), F32))
    inverse = 1.0 / (jnp.sqrt(trace) + EPS_MUON)
    square = inverse * inverse

    def scale(step, carry):
        block = gram[rows(step), :] * square
        gram[rows(step), :] = block
        low_gram[rows(step), :] = block.astype(LOW)
        return carry

    lax.fori_loop(0, tiles, scale, 0)
    ortho = moment_ref[...] * inverse
    for turn in range(ITERS_NS):

        def polynomial(step, carry):
            block = NS_B * gram[rows(step), :] + NS_C * dot(low_gram[rows(step), :], low_gram[...])
            poly[rows(step), :] = block
            low_poly[rows(step), :] = block.astype(LOW)
            return carry

        lax.fori_loop(0, tiles, polynomial, 0)
        ortho = NS_A * ortho + dot(ortho.astype(LOW), low_poly[...])
        if turn < ITERS_NS - 1:

            def mix(step, carry):
                block = (2.0 * NS_A) * poly[rows(step), :] + dot(low_poly[rows(step), :], low_poly[...])
                low_mix[rows(step), :] = block.astype(LOW)
                return carry

            lax.fori_loop(0, tiles, mix, 0)

            def advance(step, carry):
                block = (NS_A * NS_A) * gram[rows(step), :] + dot(low_gram[rows(step), :], low_mix[...])
                gram[rows(step), :] = block
                return carry

            lax.fori_loop(0, tiles, advance, 0)

            def lower(step, carry):
                low_gram[rows(step), :] = gram[rows(step), :].astype(LOW)
                return carry

            lax.fori_loop(0, tiles, lower, 0)
    step_ref[...] = (-LR_MUON * 0.2 * math.sqrt(MODEL_WIDTH)) * ortho


def newton_schulz(gram, moment, packed):
    size = moment.shape[1]
    tile = 256 if size % 256 == 0 else 128 if size % 128 == 0 else size
    big = (size, size)
    vmem = pl.BlockSpec(memory_space=pltpu.VMEM)
    flops = 2 * size * size * (7 * size + 3 * moment.shape[0])
    return pl.pallas_call(
        functools.partial(schulz_kernel, packed, tile),
        out_shape=jax.ShapeDtypeStruct(moment.shape, F32),
        in_specs=[vmem, vmem],
        out_specs=vmem,
        scratch_shapes=[
            pltpu.VMEM(big, F32),
            pltpu.VMEM(big, LOW),
            pltpu.VMEM(big, F32),
            pltpu.VMEM(big, LOW),
            pltpu.VMEM(big, LOW),
        ],
        compiler_params=pltpu.CompilerParams(vmem_limit_bytes=40 * 2**20),
        cost_estimate=pl.CostEstimate(flops=flops, bytes_accessed=3 * size * size, transcendentals=0),
        name="schulz",
    )(gram, moment)


def adam(grad, first, second):
    first_new = BETA_ONE * first + (1.0 - BETA_ONE) * grad
    second_new = BETA_TWO * second + (1.0 - BETA_TWO) * grad * grad
    corrected = first_new / (1.0 - BETA_ONE**ADAM_STEP)
    spread = jnp.sqrt(second_new / (1.0 - BETA_TWO**ADAM_STEP)) + EPS_ADAM
    return (first_new, second_new, -LR_ADAM * corrected / spread)


def shards(
    inputs,
    segment_ids,
    ancestry,
    w_query,
    key_weight,
    value_weight,
    w_output,
    w_gate,
    w_up,
    w_down,
    attn_gain,
    ffn_gain,
    cotangent,
    mom_query,
    key_momentum,
    value_momentum,
    mom_output,
    mom_gate,
    mom_up,
    mom_down,
    attn_first,
    attn_second,
    ffn_first,
    ffn_second,
):
    batches = inputs.shape[1]
    tokens = inputs.shape[2]
    tree_len = segment_ids.shape[2]
    seg_count = ancestry.shape[2]
    q_width = w_query.shape[1]
    kv_width = key_weight.shape[1]
    kv_heads = kv_width // HEAD_SIZE
    group = q_width // kv_width
    scale = 1.0 / math.sqrt(HEAD_SIZE)
    seq_size = tree_len // tokens
    inputs_share = w_gate.shape[0] // mom_gate.shape[0] // seq_size
    seq_me = lax.axis_index("seq")
    start = seq_me * tokens
    query_index = start + jnp.arange(tokens, dtype=jnp.int32)
    labels = jnp.arange(seg_count, dtype=jnp.int32)
    swap = [(0, 1), (1, 0)]
    if seq_size == 2:
        key_index = jnp.concatenate(
            [query_index, (1 - seq_me) * tokens + jnp.arange(tokens, dtype=jnp.int32)]
        )
    else:
        key_index = jnp.arange(tree_len, dtype=jnp.int32)

    def spread_keys(own):
        if seq_size == 2:
            return jnp.concatenate([own, lax.ppermute(own, "seq", swap)], axis=0)
        return lax.all_gather(own, "seq", axis=0, tiled=True)

    def collect_keys(grads):
        if seq_size == 2:
            other = lax.ppermute(grads[tokens:].astype(LOW), "seq", swap)
            return grads[:tokens] + other.astype(F32)
        return lax.psum_scatter(grads, "seq", scatter_dimension=0, tiled=True)

    queue = []

    def tensor_sum(partial):
        if queue:
            partial, queue[0] = lax.optimization_barrier((partial, queue[0]))
        total = lax.psum(partial, "tensor")
        queue[:] = [total]
        return total

    w_output_all = lax.all_gather(w_output, "tensor", axis=0, tiled=True)

    def stage_one(b):
        s = {}
        seg = segment_ids[0, b]
        member = (seg[:, None] == labels[None, :]).astype(F32)
        member_own = lax.dynamic_slice_in_dim(member, start, tokens, 0)
        if seq_size == 2:
            member_other = lax.dynamic_slice_in_dim(member, (1 - seq_me) * tokens, tokens, 0)
            member = jnp.concatenate([member_own, member_other], axis=0)
        reach = dot(member_own, ancestry[0, b].astype(F32))
        on_path = dot_nt(reach, member) > 0.5
        allowed = on_path & (query_index[:, None] >= key_index[None, :])
        positions = (jnp.sum(allowed.astype(jnp.int32), axis=1) - 1).astype(F32)
        s["allowed"] = allowed
        s["cos"], s["sin"] = rotary_tables(positions)
        resid = inputs[0, b].astype(F32)
        s["resid"] = resid
        s["scale_one"] = rms_scale(resid)
        s["plain_one"] = resid * s["scale_one"]
        s["normed_one"] = (s["plain_one"] * attn_gain).astype(LOW)
        s["query"] = rotary(dot(s["normed_one"], w_query), s["cos"], s["sin"]).astype(LOW)
        key = rotary(dot(s["normed_one"], key_weight), s["cos"], s["sin"]).astype(LOW)
        value = dot(s["normed_one"], value_weight).astype(LOW)
        s["kv"] = spread_keys(jnp.concatenate([key, value], axis=1))
        return s

    def scores_of(s):
        query_heads = s["query"].reshape(tokens, kv_heads, group, HEAD_SIZE)
        key_heads = s["kv"][:, :kv_width].reshape(tree_len, kv_heads, HEAD_SIZE)
        return (
            jnp.einsum("tkgd,skd->kgts", query_heads, key_heads, preferred_element_type=F32) * scale
        )

    def stage_two(s):
        masked = jnp.where(s["allowed"][None, None], scores_of(s), -1e30)
        top = jnp.max(masked, axis=-1, keepdims=True)
        expo = jnp.exp(masked - top)
        total = jnp.sum(expo, axis=-1, keepdims=True)
        s["logsum"] = top + jnp.log(total)
        probs = (expo / total).astype(LOW)
        value_heads = s["kv"][:, kv_width:].reshape(tree_len, kv_heads, HEAD_SIZE)
        s["mixed"] = (
            jnp.einsum("kgts,skd->tkgd", probs, value_heads, preferred_element_type=F32)
            .reshape(tokens, q_width)
            .astype(LOW)
        )
        s["mixed_all"] = lax.all_gather(s["mixed"], "tensor", axis=1, tiled=True)

    def stage_three(s, b):
        middle = s["resid"] + dot(s["mixed_all"], w_output_all)
        s["scale_two"] = rms_scale(middle)
        s["plain_two"] = middle * s["scale_two"]
        s["normed_two"] = (s["plain_two"] * ffn_gain).astype(LOW)
        gate = dot(s["normed_two"], w_gate)
        up_value = dot(s["normed_two"], w_up)
        sigma = jax.nn.sigmoid(gate)
        active = gate * sigma
        s["inner"] = (active * up_value).astype(LOW)
        block_cot = cotangent[0, b]
        inner_grad = dot_nt(block_cot, w_down)
        s["gate_grad"] = (inner_grad * up_value * sigma * (1.0 + gate * (1.0 - sigma))).astype(LOW)
        s["up_grad"] = (inner_grad * active).astype(LOW)
        two_partial = dot_nt(s["gate_grad"], w_gate) + dot_nt(s["up_grad"], w_up)
        s["two_sum"] = tensor_sum(two_partial.astype(LOW))
        s["middle"] = middle

    def stage_four(s, b):
        normed_two_grad = s["two_sum"].astype(F32)
        s["gain_two"] = jnp.sum(normed_two_grad * s["plain_two"], axis=0)
        s["middle_grad"] = cotangent[0, b].astype(F32) + norm_back(
            normed_two_grad, s["plain_two"], s["scale_two"], ffn_gain
        )
        s["middle_low"] = s["middle_grad"].astype(LOW)
        mixed_grad = dot_nt(s["middle_low"], w_output).astype(LOW)
        probs_full = jnp.exp(
            jnp.where(s["allowed"][None, None], scores_of(s), -1e30) - s["logsum"]
        )
        probs_low = probs_full.astype(LOW)
        mixed_heads = mixed_grad.reshape(tokens, kv_heads, group, HEAD_SIZE)
        value_heads = s["kv"][:, kv_width:].reshape(tree_len, kv_heads, HEAD_SIZE)
        key_heads = s["kv"][:, :kv_width].reshape(tree_len, kv_heads, HEAD_SIZE)
        query_heads = s["query"].reshape(tokens, kv_heads, group, HEAD_SIZE)
        prob_grad = jnp.einsum("tkgd,skd->kgts", mixed_heads, value_heads, preferred_element_type=F32)
        value_grad = jnp.einsum(
            "kgts,tkgd->skd", probs_low, mixed_heads, preferred_element_type=F32
        ).reshape(tree_len, kv_width)
        score_grad = (
            probs_full * (prob_grad - jnp.sum(probs_full * prob_grad, axis=-1, keepdims=True))
        ).astype(LOW)
        query_grad = (
            jnp.einsum("kgts,skd->tkgd", score_grad, key_heads, preferred_element_type=F32).reshape(
                tokens, q_width
            )
            * scale
        )
        key_grad = (
            jnp.einsum("kgts,tkgd->skd", score_grad, query_heads, preferred_element_type=F32).reshape(
                tree_len, kv_width
            )
            * scale
        )
        kv_grad = collect_keys(jnp.concatenate([key_grad, value_grad], axis=1))
        s["query_low"] = rotary(query_grad, s["cos"], -s["sin"]).astype(LOW)
        s["key_low"] = rotary(kv_grad[:, :kv_width], s["cos"], -s["sin"]).astype(LOW)
        s["value_low"] = kv_grad[:, kv_width:].astype(LOW)
        one_partial = (
            dot_nt(s["query_low"], w_query)
            + dot_nt(s["key_low"], key_weight)
            + dot_nt(s["value_low"], value_weight)
        )
        s["ffn_sum"] = tensor_sum(dot(s["inner"], w_down).astype(LOW))
        s["one_sum"] = tensor_sum(one_partial.astype(LOW))

    def stage_five(s):
        normed_one_grad = s["one_sum"].astype(F32)
        s["gain_one"] = jnp.sum(normed_one_grad * s["plain_one"], axis=0)
        s["block_out"] = s["middle"] + s["ffn_sum"].astype(F32)
        s["input_grad"] = s["middle_grad"] + norm_back(
            normed_one_grad, s["plain_one"], s["scale_one"], attn_gain
        )

    def weight_grad(lefts, rights):
        total = dot_tn(lefts[0], rights[0])
        for left, right in zip(lefts[1:], rights[1:]):
            total = total + dot_tn(left, right)
        return total.astype(LOW)

    def column(name):
        return [s[name] for s in states]

    sizes = (seq_size, inputs_share)

    def finish(grads, olds, name, number):
        sums = exchange(grads, sizes, name + "_grads", number)
        moments = [MU_MUON * old + total for old, total in zip(olds, sums)]
        return sums, moments

    def gram_of(moment):
        low = moment.astype(LOW)
        return dot_tn(low, low).astype(LOW)

    def packed_gram(moment):
        low = moment.astype(LOW)
        half = low.shape[1] // 2
        front, back = low[:, :half], low[:, half:]
        return [dot_tn(front, front), dot_tn(front, back), dot_tn(back, back)]

    states = [stage_one(b) for b in range(batches)]
    for s in states:
        stage_two(s)
    for b, s in enumerate(states):
        stage_three(s, b)
    cots = [cotangent[0, b] for b in range(batches)]
    ffn_grads = [
        weight_grad(column("normed_two"), column("gate_grad")),
        weight_grad(column("normed_two"), column("up_grad")),
        weight_grad(cots, column("inner")),
    ]
    for b, s in enumerate(states):
        stage_four(s, b)
    ffn_sums, ffn_moments = finish(ffn_grads, [mom_gate, mom_up, mom_down.T], "ffn", 0)
    half = ffn_moments[0].shape[1] // 2
    grams = jnp.concatenate(
        [jnp.concatenate(packed_gram(m), axis=0).astype(LOW) for m in ffn_moments], axis=1
    )
    (grams,) = exchange([grams], sizes, "ffn_grams", 1, gather=True)
    ffn_steps = [
        newton_schulz(
            grams[:, i * half : (i + 1) * half].reshape(3, half, half), ffn_moments[i], True
        )
        for i in range(3)
    ]
    attn_grads = [
        weight_grad(column("normed_one"), column("query_low")),
        weight_grad(column("normed_one"), column("key_low")),
        weight_grad(column("normed_one"), column("value_low")),
        weight_grad(column("middle_low"), column("mixed")),
    ]
    for s in states:
        stage_five(s)
    attn_sums, attn_moments = finish(
        attn_grads, [mom_query, key_momentum, value_momentum, mom_output.T], "attn", 2
    )
    pair = jnp.concatenate([gram_of(attn_moments[1]), gram_of(attn_moments[2])], axis=1)
    grams = jnp.concatenate([gram_of(attn_moments[0]), gram_of(attn_moments[3]), pair], axis=0)
    (grams,) = exchange([grams], sizes, "attn_grams", 3, gather=True)
    attn_steps = [
        newton_schulz(grams[:q_width], attn_moments[0], False),
        newton_schulz(grams[2 * q_width :, :kv_width], attn_moments[1], False),
        newton_schulz(grams[2 * q_width :, kv_width:], attn_moments[2], False),
        newton_schulz(grams[q_width : 2 * q_width], attn_moments[3], False),
    ]
    gains = jnp.stack([sum(column("gain_one")), sum(column("gain_two"))])
    gains = lax.psum(gains, ("dp", "seq"))
    attn_total, ffn_total = gains[0], gains[1]
    outputs = jnp.stack(column("block_out"))
    input_grads = jnp.stack(column("input_grad"))
    attn_one, attn_two, attn_step = adam(attn_total, attn_first, attn_second)
    ffn_one, ffn_two, ffn_step = adam(ffn_total, ffn_first, ffn_second)

    def listed(attn, ffn):
        return (attn[0], attn[1], attn[2], attn[3].T, ffn[0], ffn[1], ffn[2].T)

    return (
        (outputs[None], input_grads[None])
        + listed(attn_sums, ffn_sums)
        + (attn_total, ffn_total)
        + listed(attn_moments, ffn_moments)
        + listed(attn_steps, ffn_steps)
        + (attn_one, attn_two, attn_step, ffn_one, ffn_two, ffn_step)
    )


def solution(mesh):
    tokens = P("dp", None, "seq", None)
    column_split = P(None, "tensor")
    row_split = P("tensor", None)
    standing = P(("dp", "seq"), "tensor")
    lying = P("tensor", ("dp", "seq"))
    seven = (standing, standing, standing, lying, standing, standing, lying)
    placed = (
        (tokens, P("dp", None, None), P("dp", None, None, None))
        + (column_split, column_split, column_split, row_split)
        + (column_split, column_split, row_split)
        + (P(), P(), tokens)
        + seven
        + (P(), P(), P(), P())
    )
    results = (tokens, tokens) + seven + (P(), P()) + seven + seven + (P(),) * 6
    return jax.shard_map(shards, mesh=mesh, in_specs=placed, out_specs=results, check_vma=False)
```

time: 2100 us -> 940 us (0.45)
  waiting for transfers between devices: 1330 us -> 385 us
  matrix products: 469 us -> 156 us
  Pallas kernels: 0 us -> 242 us
  local copies, waits for them, and re-layouts: 96 us -> 42.1 us
  other arithmetic: 104 us -> 59.5 us
  blocking collectives: 54.6 us -> 23.9 us
    psum x12 -> x6, waiting for transfers between devices: 962 us -> 242 us  [tensor_sum(): total = lax.psum(partial, 'tensor')]
    reduce_scatter x11 -> x0, waiting for transfers between devices: 370 us -> none  [the longest x1 63.9 us: shards(): lax.psum_scatter(grads[5], ('dp', 'seq'), scatter_dimension=0, tiled=True)]
    dot_general x159 -> x67, matrix products: 466 us -> 152 us  [the longest x14 43.7 us: dot(): return jnp.dot(left, right, preferred_element_type=F32)]
    pallas_call x0 -> x11, Pallas kernels: none -> 242 us  [the longest x4 148 us: exchange(): pl.pallas_call(functools.partial(exchange_kernel, count, bits, seq_bits,...]
    all_gather x0 -> x3, waiting for transfers between devices: none -> 128 us  [the longest x1 89.9 us: shards(): w_output_all = lax.all_gather(w_output, 'tensor', axis=0, tiled=True)]
    while x232 -> x0, local copies, waits for them, and re-layouts: 54 us -> none
    all_gather x4 -> x0, blocking collectives: 29.4 us -> none  [the longest x2 16.2 us: micro(): lax.all_gather(value_own, 'seq', axis=0, tiled=True)]
    unnamed x247 -> x264, local copies, waits for them, and re-layouts: 2.97 us -> 27.2 us
  transfers between devices with their start and end apart: 23 -> 13, of which waited for: 19 -> 12; matrix products, arithmetic and copies ran while one was open for 18% -> 8% of each run, Pallas kernels for 0% -> 15%
where the time goes in v1:
time: 940 us; the launch traced here: 932 us
  waiting for transfers between devices  385 us (41%)
  Pallas kernels  242 us (26%)
  matrix products  156 us (17%)
  other arithmetic  59.5 us (6%)
  local copies, waits for them, and re-layouts  42.1 us (4%)
  blocking collectives  23.9 us (3%)
  between operations  15.9 us (2%)
    psum x6, waiting for transfers between devices, tensor_sum(): total = lax.psum(partial, 'tensor')  242 us
    pallas_call x4, Pallas kernels, exchange(): pl.pallas_call(functools.partial(exchange_kernel, count, bits, seq_bits,...  148 us
    pallas_call x7, Pallas kernels, newton_schulz(): pl.pallas_call(functools.partial(schulz_kernel, packed, tile), out_shape=...  94.4 us
    all_gather x1, waiting for transfers between devices, shards(): w_output_all = lax.all_gather(w_output, 'tensor', axis=0, tiled=True)  89.9 us
    dot_general x14, matrix products, dot(): return jnp.dot(left, right, preferred_element_type=F32)  43.7 us
    dot_general x27, matrix products, dot_tn(): lax.dot_general(left, right, (((0,), (0,)), ((), ())), preferred_element_...  41.7 us
    all_gather x2, waiting for transfers between devices, stage_two(): s['mixed_all'] = lax.all_gather(s['mixed'], 'tensor', axis=1, tiled=True)  38.6 us
    dot_general x16, matrix products, dot_nt(): lax.dot_general(left, right, (((1,), (1,)), ((), ())), preferred_element_...  37 us
  transfers between devices with their start and end apart: 13, of which 12 were waited for; matrix products, arithmetic and copies ran while one was open for 8% of the time, Pallas kernels for 15%

profile of v1, /device:TPU:0, one launch (start us, length us, event | category | flops | bytes accessed | tf_op | source)
XLA Modules:
  0.0 931.7 jit_solution(10614899070325909204)
XLA Ops:
  12.5 2.7 fusion.56
  21.3 3.0 collective-permute-start
  24.3 2.4 copy.90
  26.6 3.5 fusion.88
  30.1 2.3 copy.89
  43.7 2.4 fusion.81
  51.1 2.4 copy.93
  54.8 4.0 collective-permute-done.1
  63.0 2.3 fusion.98
  65.6 5.5 fusion.77
  72.3 8.7 all-gather.4.cloned.1.call-done
  81.0 89.9 %all-gather.6.cloned.1.call-done = bf16[1536,1536]{1,0:T(8,128)(2,1)} async-done(((bf16[384,1536]{1,0:T(8,128)(2,1)}), bf16[1536,1536]{1,0:T(8,128)(2,1)}) %all-gather.6.cloned.1.call-update) | async-done | bytes 4718608 | tf_op jit(solution)/shard_map/all_gather | solution.py:420
  170.8 7.7 multiply_reduce_fusion.1
  178.5 29.9 %all-gather.8.cloned.1.call-done = bf16[512,1536]{0,1:T(8,128)(2,1)} async-done(((bf16[512,384]{0,1:T(8,128)(2,1)}), bf16[512,1536]{0,1:T(8,128)(2,1)}) %all-gather.8.cloned.1.call-update) | async-done | bytes 1572880 | tf_op jit(solution)/shard_map/all_gather | solution.py:467
  208.5 6.4 multiply_reduce_fusion
  223.9 2.6 multiply_convert_fusion.7
  226.5 5.0 fusion.206
  231.5 4.5 fusion.205
  237.9 4.0 multiply_convert_fusion.5
  242.8 3.7 fusion.38
  246.5 4.8 copy.103
  251.3 7.2 add_convert_fusion.1
  258.5 4.6 add_convert_fusion.2
  263.1 47.2 %ffn_grads.1 = (f32[192,1024]{1,0:T(8,128)S(1)}, f32[192,1024]{1,0:T(8,128)S(1)}, f32[192,1024]{1,0:T(8,128)S(1)}) custom-call(bf16[2,2,2,192,1024]{4,3,2,1,0:T(8,128)(2,1)S(1)} %bitcast.332, bf16[2,2,2,192,1024]{4,3,2,1,0:T(8,128)(2,1)} %bitcast.364, bf16[2,2,2,192,1024]{4,3,2,1,0:T(8,128)(2,1)} %bitcast.347), custom_call_target="tpu_custom_call" | custom-call | bytes 150994944 | tf_op jit(solution)/shard_map/ffn_grads/pallas_call | solution.py:230
  316.6 3.5 fusion.202
  320.1 3.5 fusion.201
  323.9 2.4 pad_maximum_fusion.refs_0_
  326.3 55.3 %ffn_grams.1 = bf16[2,2,2,192,1536]{4,3,2,1,0:T(8,128)(2,1)S(1)} custom-call(bf16[2,2,2,192,1536]{4,3,2,1,0:T(8,128)(2,1)} %pad_maximum_fusion.refs_0_), custom_call_target="tpu_custom_call" | custom-call | bytes 75497472 | tf_op jit(solution)/shard_map/ffn_grams/pallas_call | solution.py:230
  381.6 2.5 fusion.181
  385.5 3.0 fusion.66
  391.1 25.6 %schulz.13 = f32[192,1024]{1,0:T(8,128)} custom-call(bf16[3,512,512]{2,1,0:T(8,128)(2,1)S(1)} %bitcast.338, f32[192,1024]{1,0:T(8,128)S(1)} %copy-done.26), custom_call_target="tpu_custom_call" | custom-call | flops 16240345088 | bytes 3145728 | tf_op jit(solution)/shard_map/schulz/pallas_call | solution.py:325
  416.7 3.0 fusion.65
  422.2 25.8 %schulz.12 = f32[192,1024]{1,0:T(8,128)} custom-call(bf16[3,512,512]{2,1,0:T(8,128)(2,1)S(1)} %bitcast.337, f32[192,1024]{1,0:T(8,128)S(1)} %copy-done.25), custom_call_target="tpu_custom_call" | custom-call | flops 16240345088 | bytes 3145728 | tf_op jit(solution)/shard_map/schulz/pallas_call | solution.py:325
  448.0 9.3 all-reduce.7.cloned.1.call-done
  457.4 5.3 convolution_convert_fusion.1
  462.7 25.4 %schulz.11 = f32[192,1024]{1,0:T(8,128)} custom-call(bf16[3,512,512]{2,1,0:T(8,128)(2,1)S(1)} %bitcast.336, f32[192,1024]{1,0:T(8,128)S(1)} %copy-done.24), custom_call_target="tpu_custom_call" | custom-call | flops 16240345088 | bytes 3145728 | tf_op jit(solution)/shard_map/schulz/pallas_call | solution.py:325
  488.0 40.3 %all-reduce.9.cloned.1.call-done = bf16[512,1536]{1,0:T(8,128)(2,1)} async-done(((bf16[512,1536]{1,0:T(8,128)(2,1)}), bf16[512,1536]{1,0:T(8,128)(2,1)}) %all-reduce.9.cloned.1.call-update) | async-done | bytes 1572880 | tf_op jit(solution)/shard_map/psum | solution.py:416
  528.4 5.4 convolution_convert_fusion
  533.8 4.2 fusion.52
  538.0 61.2 %all-reduce.11.cloned.1.call-done = bf16[512,1536]{1,0:T(8,128)(2,1)} async-done(((bf16[512,1536]{1,0:T(8,128)(2,1)}), bf16[512,1536]{1,0:T(8,128)(2,1)}) %all-reduce.11.cloned.1.call-update) | async-done | bytes 1572880 | tf_op jit(solution)/shard_map/psum | solution.py:416
  599.3 6.4 fusion.44
  606.9 9.3 fusion
  616.1 5.0 fusion.10
  624.8 5.1 fusion.3
  629.9 5.1 fusion.2
  637.3 4.7 fusion.5
  650.1 2.7 fusion.204
  656.2 3.6 collective-permute-done.3
  660.6 5.8 collective-permute-done.2
  673.2 2.4 fusion.71
  677.5 22.0 %attn_grads.1 = (f32[192,384]{1,0:T(8,128)S(1)}, f32[192,192]{1,0:T(8,128)S(1)}, f32[192,192]{1,0:T(8,128)S(1)}, f32[192,384]{1,0:T(8,128)S(1)}) custom-call(bf16[2,2,2,192,384]{4,3,2,1,0:T(8,128)(2,1)S(1)} %bitcast.341, bf16[2,2,2,192,192]{4,3,2,1,0:T(8,128)(2,1)S(1)} %bitcast.334, bf16[2,2,2,192,192]{4,3,2,1,0:T(8,128)(2,1)S(1)} %bitcast.333, ...), custom_call_target="tpu_custom_call" | custom-call | bytes 56623104 | tf_op jit(solution)/shard_map/attn_grads/pallas_call | solution.py:230
  700.4 41.0 %all-reduce.13.cloned.1.call-done = bf16[512,1536]{1,0:T(8,128)(2,1)} async-done(((bf16[512,1536]{1,0:T(8,128)(2,1)}), bf16[512,1536]{1,0:T(8,128)(2,1)}) %all-reduce.13.cloned.1.call-update) | async-done | bytes 1572880 | tf_op jit(solution)/shard_map/psum | solution.py:416
  742.2 23.2 %attn_grams.1 = bf16[2,2,2,120,384]{4,3,2,1,0:T(8,128)(2,1)S(1)} custom-call(bf16[2,2,2,120,384]{4,3,2,1,0:T(8,128)(2,1)S(1)} %bitcast.335), custom_call_target="tpu_custom_call" | custom-call | bytes 11796480 | tf_op jit(solution)/shard_map/attn_grams/pallas_call | solution.py:230
  765.5 2.4 schulz.9
  767.9 2.4 schulz.8
  773.7 38.3 %all-reduce.15.cloned.1.call-done = bf16[512,1536]{1,0:T(8,128)(2,1)} async-done(((bf16[512,1536]{1,0:T(8,128)(2,1)}), bf16[512,1536]{1,0:T(8,128)(2,1)}) %all-reduce.15.cloned.1.call-update) | async-done | bytes 1572880 | tf_op jit(solution)/shard_map/psum | solution.py:416
  812.1 6.5 schulz.10
  818.6 6.5 schulz.7
  827.0 3.1 maximum_bitcast_fusion
  830.1 52.4 %all-reduce.17.cloned.1.call-done = bf16[512,1536]{1,0:T(8,128)(2,1)} async-done(((bf16[512,1536]{1,0:T(8,128)(2,1)}), bf16[512,1536]{1,0:T(8,128)(2,1)}) %all-reduce.17.cloned.1.call-update) | async-done | bytes 1572880 | tf_op jit(solution)/shard_map/psum | solution.py:416
  882.5 3.8 fusion.55
  886.4 23.9 %psum.55 = f32[2,1536]{1,0:T(2,128)S(1)} all-reduce(f32[2,1536]{1,0:T(2,128)S(1)} %pad_maximum_fusion.14), channel_id=1, replica_groups=mesh['dp'=4,'seq'=2,'tensor'=4] {'dp','seq'}, use_global_device_ids=true, to_apply=%region_26.27 | all-reduce | flops 3072 | bytes 24576 | tf_op jit(solution)/shard_map/psum | solution.py:614
  910.3 4.6 fusion.47
  915.1 3.2 maximum_bitcast_fusion.1
  (408 shorter events, 100.6 us)
Async XLA Ops:
  7.2 214.9 %copy-start = (bf16[1536,1024]{1,0:T(8,128)(2,1)S(1)}, bf16[1536,1024]{1,0:T(8,128)(2,1)}, u32[]{:S(2)}) copy-start(bf16[1536,1024]{1,0:T(8,128)(2,1)} %param.32) | copy-start | bytes 9437188
  7.2 73.8 %all-gather.4.cloned.1.call-start = ((), (), s32[]{:S(2)}) async-start(), calls=%async_computation | async-start | bytes 1966080 | tf_op jit(solution)/shard_map/all_gather | solution.py:467
  15.8 10.9 %copy-start.104 = (f32[512]{0:T(512)}, f32[512]{0:T(512)S(1)}, u32[]{:S(2)}) copy-start(f32[512]{0:T(512)S(1)} %get-tuple-element.161) | copy-start | bytes 6148
  19.8 12.7 %copy-start.46 = (f32[512,48]{0,1:T(8,128)}, f32[512,48]{0,1:T(8,128)S(1)}, u32[]{:S(2)}) copy-start(f32[512,48]{0,1:T(8,128)S(1)} %get-tuple-element.141) | copy-start | bytes 294916
  19.8 33.6 %copy-start.48 = (f32[512,48]{0,1:T(8,128)}, f32[512,48]{0,1:T(8,128)S(1)}, u32[]{:S(2)}) copy-start(f32[512,48]{0,1:T(8,128)S(1)} %get-tuple-element.136) | copy-start | bytes 294916
  21.3 12.6 %collective-permute-start = (bf16[512,384]{0,1:T(8,128)(2,1)}, bf16[512,384]{0,1:T(8,128)(2,1)}, u32[]{:S(2)}, u32[]{:S(2)}) collective-permute-start(bf16[512,384]{0,1:T(8,128)(2,1)} %pad_maximum_fusion.8), channel_id=1, source_target_pairs={{0,4},{4,0},{1,5},{5,1},{2,6},{6,2},{3,7},{7,3},{8,12},{12,8},{9,1... | collective-permute-start | bytes 1179656 | tf_op jit(solution)/shard_map/ppermute | solution.py:402
  42.7 128.2 %all-gather.6.cloned.1.call-start = ((), (), s32[]{:S(2)}) async-start(), calls=%async_computation.1 | async-start | bytes 5898240 | tf_op jit(solution)/shard_map/all_gather | solution.py:420
  43.4 165.0 %all-gather.8.cloned.1.call-start = ((), (), s32[]{:S(2)}) async-start(), calls=%async_computation.2 | async-start | bytes 1966080 | tf_op jit(solution)/shard_map/all_gather | solution.py:467
  47.9 10.9 %collective-permute-start.1 = (bf16[512,384]{0,1:T(8,128)(2,1)}, bf16[512,384]{0,1:T(8,128)(2,1)}, u32[]{:S(2)}, u32[]{:S(2)}) collective-permute-start(bf16[512,384]{0,1:T(8,128)(2,1)} %pad_maximum_fusion.10), channel_id=1, source_target_pairs={{0,4},{4,0},{1,5},{5,1},{2,6},{6,2},{3,7},{7,3},{8,12},{12,8},{9,1... | collective-permute-start | bytes 1179656 | tf_op jit(solution)/shard_map/ppermute | solution.py:402
  53.4 6.6 copy-start.86
  54.8 7.0 copy-start.63
  65.3 6.4 copy-start.99
  65.3 391.9 %all-reduce.7.cloned.1.call-start = ((), (), s32[]{:S(2)}) async-start(), calls=%async_computation.3 | async-start | bytes 3145728 | tf_op jit(solution)/shard_map/psum | solution.py:416
  178.5 36.3 %copy-start.93 = (f32[1536]{0:T(1024)S(1)}, f32[1536]{0:T(1024)}, u32[]{:S(2)}) copy-start(f32[1536]{0:T(1024)} %param.35) | copy-start | bytes 18436
  208.5 6.4 copy-start.35
  216.5 5.5 copy-start.56
  226.5 9.5 %copy-start.114 = (bf16[512,1024]{1,0:T(8,128)(2,1)}, bf16[512,1024]{1,0:T(8,128)(2,1)S(1)}, u32[]{:S(2)}) copy-start(bf16[512,1024]{1,0:T(8,128)(2,1)S(1)} %get-tuple-element.87) | copy-start | bytes 3145732
  251.3 7.2 copy-start.57
  251.3 7.2 copy-start.120
  263.1 47.2 %copy-start.82 = (f32[192,1024]{1,0:T(8,128)S(1)}, f32[192,1024]{1,0:T(8,128)}, u32[]{:S(2)}) copy-start(f32[192,1024]{1,0:T(8,128)} %param.41) | copy-start | bytes 2359300
  388.5 139.8 %all-reduce.9.cloned.1.call-start = ((), (), s32[]{:S(2)}) async-start(), calls=%async_computation.4 | async-start | bytes 3145728 | tf_op jit(solution)/shard_map/psum | solution.py:416
  391.1 25.6 %copy-start.119 = (bf16[512,1024]{1,0:T(8,128)(2,1)S(1)}, bf16[512,1024]{1,0:T(8,128)(2,1)}, u32[]{:S(2)}) copy-start(bf16[512,1024]{1,0:T(8,128)(2,1)} %get-tuple-element.84) | copy-start | bytes 3145732
  391.1 25.6 %copy-start.121 = (f32[512,1536]{1,0:T(8,128)S(1)}, f32[512,1536]{1,0:T(8,128)}, u32[]{:S(2)}) copy-start(f32[512,1536]{1,0:T(8,128)} %fusion.201) | copy-start | bytes 9437188
  457.3 5.4 copy-start.8
  457.3 5.4 copy-start.24
  457.3 141.9 %all-reduce.11.cloned.1.call-start = ((), (), s32[]{:S(2)}) async-start(), calls=%async_computation.5 | async-start | bytes 3145728 | tf_op jit(solution)/shard_map/psum | solution.py:416
  528.3 5.4 copy-start.30
  528.3 213.1 %all-reduce.13.cloned.1.call-start = ((), (), s32[]{:S(2)}) async-start(), calls=%async_computation.6 | async-start | bytes 3145728 | tf_op jit(solution)/shard_map/psum | solution.py:416
  599.3 6.4 copy-start.41
  605.6 16.6 %copy-start.34 = (f32[512,1536]{1,0:T(8,128)}, f32[512,1536]{1,0:T(8,128)S(1)}, u32[]{:S(2)}) copy-start(f32[512,1536]{1,0:T(8,128)S(1)} %get-tuple-element.93) | copy-start | bytes 9437188
  605.6 49.5 %copy-start.32 = (f32[512,1536]{1,0:T(8,128)}, f32[512,1536]{1,0:T(8,128)S(1)}, u32[]{:S(2)}) copy-start(f32[512,1536]{1,0:T(8,128)S(1)} %get-tuple-element.92) | copy-start | bytes 9437188
  616.1 6.9 slice-start
  623.3 6.5 slice-start.2
  624.8 5.1 slice-start.3
  629.9 5.1 copy-start.64
  647.7 12.1 %collective-permute-start.3 = (bf16[512,384]{0,1:T(8,128)(2,1)S(1)}, bf16[512,384]{0,1:T(8,128)(2,1)S(1)}, u32[]{:S(2)}, u32[]{:S(2)}) collective-permute-start(bf16[512,384]{0,1:T(8,128)(2,1)S(1)} %fusion.112), channel_id=1, source_target_pairs={{0,4},{4,0},{1,5},{5,1},{2,6},{6,2},{3,7},{7,3},{8,12},{12,8},{9,1... | collective-permute-start | bytes 1179656 | tf_op jit(solution)/shard_map/ppermute | solution.py:407
  649.4 17.0 %collective-permute-start.2 = (bf16[512,384]{0,1:T(8,128)(2,1)S(1)}, bf16[512,384]{0,1:T(8,128)(2,1)S(1)}, u32[]{:S(2)}, u32[]{:S(2)}) collective-permute-start(bf16[512,384]{0,1:T(8,128)(2,1)S(1)} %fusion.113), channel_id=1, source_target_pairs={{0,4},{4,0},{1,5},{5,1},{2,6},{6,2},{3,7},{7,3},{8,12},{12,8},{9,1... | collective-permute-start | bytes 1179656 | tf_op jit(solution)/shard_map/ppermute | solution.py:407
  659.9 6.5 copy-start.44
  672.3 139.7 %all-reduce.15.cloned.1.call-start = ((), (), s32[]{:S(2)}) async-start(), calls=%async_computation.7 | async-start | bytes 3145728 | tf_op jit(solution)/shard_map/psum | solution.py:416
  675.7 23.9 %copy-start.89 = (f32[192,192]{1,0:T(8,128)S(1)}, f32[192,192]{1,0:T(8,128)}, u32[]{:S(2)}) copy-start(f32[192,192]{1,0:T(8,128)} %param.39) | copy-start | bytes 442372
  677.5 22.3 %copy-start.87 = (f32[384,192]{0,1:T(8,128)S(1)}, f32[384,192]{0,1:T(8,128)}, u32[]{:S(2)}) copy-start(f32[384,192]{0,1:T(8,128)} %param.40) | copy-start | bytes 884740
  677.5 22.7 %copy-start.90 = (f32[192,192]{1,0:T(8,128)S(1)}, f32[192,192]{1,0:T(8,128)}, u32[]{:S(2)}) copy-start(f32[192,192]{1,0:T(8,128)} %param.38) | copy-start | bytes 442372
  677.5 22.8 %copy-start.88 = (f32[192,384]{1,0:T(8,128)S(1)}, f32[192,384]{1,0:T(8,128)}, u32[]{:S(2)}) copy-start(f32[192,384]{1,0:T(8,128)} %param.37) | copy-start | bytes 884740
  699.5 42.5 %copy-start.13 = (f32[192,384]{1,0:T(8,128)}, f32[192,384]{1,0:T(8,128)S(1)}, u32[]{:S(2)}) copy-start(f32[192,384]{1,0:T(8,128)S(1)} %get-tuple-element.51) | copy-start | bytes 884740
  699.6 65.9 %copy-start.18 = (f32[192,192]{1,0:T(8,128)}, f32[192,192]{1,0:T(8,128)S(1)}, u32[]{:S(2)}) copy-start(f32[192,192]{1,0:T(8,128)S(1)} %multiply_add_fusion.5.moment_ref) | copy-start | bytes 442372
  699.9 112.2 %copy-start.11 = (f32[192,384]{1,0:T(8,128)}, f32[192,384]{1,0:T(8,128)S(1)}, u32[]{:S(2)}) copy-start(f32[192,384]{1,0:T(8,128)S(1)} %bitcast_add_fusion.1.moment_ref) | copy-start | bytes 884740
  700.3 67.6 %copy-start.19 = (f32[192,192]{1,0:T(8,128)}, f32[192,192]{1,0:T(8,128)S(1)}, u32[]{:S(2)}) copy-start(f32[192,192]{1,0:T(8,128)S(1)} %multiply_add_fusion.6.moment_ref) | copy-start | bytes 442372
  700.4 118.2 %copy-start.12 = (f32[192,384]{1,0:T(8,128)}, f32[192,384]{1,0:T(8,128)S(1)}, u32[]{:S(2)}) copy-start(f32[192,384]{1,0:T(8,128)S(1)} %multiply_add_fusion.4.moment_ref) | copy-start | bytes 884740
  700.4 69.9 %copy-start.51 = (bf16[1536,192]{0,1:T(8,128)(2,1)S(1)}, bf16[1536,192]{0,1:T(8,128)(2,1)}, u32[]{:S(2)}) copy-start(bf16[1536,192]{0,1:T(8,128)(2,1)} %param.28) | copy-start | bytes 1769476
  741.5 141.0 %all-reduce.17.cloned.1.call-start = ((), (), s32[]{:S(2)}) async-start(), calls=%async_computation.8 | async-start | bytes 3145728 | tf_op jit(solution)/shard_map/psum | solution.py:416
  741.5 28.7 %copy-start.39 = (f32[512,1536]{1,0:T(8,128)S(1)}, f32[512,1536]{1,0:T(8,128)}, u32[]{:S(2)}) copy-start(f32[512,1536]{1,0:T(8,128)} %fusion.204) | copy-start | bytes 9437188
  812.1 13.0 %copy-start.31 = (f32[512,1536]{1,0:T(8,128)S(1)}, f32[512,1536]{1,0:T(8,128)}, u32[]{:S(2)}) copy-start(f32[512,1536]{1,0:T(8,128)} %copy-done.29) | copy-start | bytes 9437188
  812.1 13.0 %copy-start.60 = (bf16[512,1536]{1,0:T(8,128)(2,1)S(1)}, bf16[512,1536]{1,0:T(8,128)(2,1)}, u32[]{:S(2)}) copy-start(bf16[512,1536]{1,0:T(8,128)(2,1)} %all-reduce.15.cloned.1.call-done) | copy-start | bytes 4718596
  827.0 55.5 %copy-start.103 = (f32[512]{0:T(512)S(1)}, f32[512]{0:T(512)}, u32[]{:S(2)}) copy-start(f32[512]{0:T(512)} %get-tuple-element.160) | copy-start | bytes 6148
  827.0 55.5 %copy-start.106 = (f32[512]{0:T(512)S(1)}, f32[512]{0:T(512)}, u32[]{:S(2)}) copy-start(f32[512]{0:T(512)} %copy-done.104) | copy-start | bytes 6148
  830.1 80.2 %copy-start.33 = (f32[512,1536]{1,0:T(8,128)S(1)}, f32[512,1536]{1,0:T(8,128)}, u32[]{:S(2)}) copy-start(f32[512,1536]{1,0:T(8,128)} %copy-done.32) | copy-start | bytes 9437188
  910.3 8.0 copy-start.97
  910.3 8.6 copy-start.96
  915.1 5.2 copy-start.23
  915.1 5.9 copy-start.21
  915.1 6.5 copy-start.14
  915.1 7.2 copy-start.7
  918.3 5.8 copy-start.3
  919.5 5.4 copy-start.1
  (78 other events, 195.0 us)
Sparse Core Ops, SparseCore 0:
  42.8 38.1 all-gather.3
  82.6 88.2 all-gather.5
  173.0 35.4 all-gather.7
  388.6 68.5 all-reduce.6
  460.1 68.1 all-reduce.8
  531.1 68.1 all-reduce.10
  672.4 68.9 all-reduce.12
  743.8 68.1 all-reduce.14
  814.3 68.1 all-reduce.16

commit v2 on v1

--- a/solution.py
+++ b/solution.py
@@ -86,26 +86,35 @@
     return {axis: lax.axis_index(axis) + power * (1 - 2 * my_bit(bit, seq_bits))}
 
 
-def exchange_kernel(count, bits, seq_bits, chunks, gather, *refs):
-    sources, outs, refs = refs[:count], refs[count : 2 * count], refs[2 * count :]
+def exchange_kernel(gathers, bits, seq_bits, chunks, lanes, pieces, lag, *refs):
+    count, sums = len(gathers), 2 if pieces else 0
+    sources, zin, refs = refs[:count], refs[count : count + sums], refs[count + sums :]
+    outs, zout, refs = refs[:count], refs[count : count + sums], refs[count + sums :]
     held = [refs[stage * count : (stage + 1) * count] for stage in range(bits)]
     refs = refs[bits * count :]
-    if gather:
-        whole, refs = refs[:count], refs[count:]
-    send_sem, recv_sem, out_sem = refs
+    whole, refs = refs[:count], refs[count:]
+    send_sem, recv_sem, out_sem = refs[:3]
     every = list(range(bits - 1, -1, -1))
     core = min(seq_bits, bits - 1)
     rest = [bit for bit in every if bit != core]
     me = {bit: my_bit(bit, seq_bits) for bit in every}
     there = {bit: partner_of(bit, seq_bits) for bit in every}
     copies = []
+    mesh_ids = pl.DeviceIdType.MESH
 
     barrier = pltpu.get_barrier_semaphore()
     for bit in every:
-        pl.semaphore_signal(
-            barrier, inc=1, device_id=there[bit], device_id_type=pl.DeviceIdType.MESH
-        )
-    pl.semaphore_wait(barrier, bits)
+        pl.semaphore_signal(barrier, inc=1, device_id=there[bit], device_id_type=mesh_ids)
+    if sums:
+        spot_z = lax.axis_index("tensor")
+        for shift in (1, lanes - 1):
+            pl.semaphore_signal(
+                barrier,
+                inc=1,
+                device_id={"tensor": (spot_z + shift) % lanes},
+                device_id_type=mesh_ids,
+            )
+    pl.semaphore_wait(barrier, bits + (2 if sums else 0))
 
     def order_of(number):
         turn = number % len(rest)
@@ -121,14 +130,16 @@
             send_sem=send_sem.at[slot, number],
             recv_sem=recv_sem.at[slot, number],
             device_id=there[bit],
-            device_id_type=pl.DeviceIdType.MESH,
+            device_id_type=mesh_ids,
         )
         copy.start()
         copies.append(copy)
         return copy
 
     arriving = {}
-    for number, (index, columns) in enumerate(chunks):
+
+    def halve_first(number):
+        index, columns = chunks[number]
         left = list(every)
         source = sources[index].at[place(left, {core: 1 - me[core]}, columns)]
         left.remove(core)
@@ -148,56 +159,175 @@
             total = total + held[past][index][place(left, known, columns)].astype(F32)
         return total
 
-    for stage in range(1, bits):
-        for number, (index, columns) in enumerate(chunks):
-            order = order_of(number)
-            bit = order[stage]
-            arriving[number].wait_recv()
-            left = [b for b in every if b not in order[:stage]]
-            spot = place(left, {bit: 1 - me[bit]}, columns)
-            held[stage - 1][index][spot] = summed(number, stage, {bit: 1 - me[bit]}).astype(LOW)
-            left.remove(bit)
-            target = held[stage][index].at[place(left, {}, columns)]
-            arriving[number] = send(held[stage - 1][index].at[spot], target, stage, number, bit)
-
-    for number, (index, columns) in enumerate(chunks):
+    def halve(number, stage):
+        index, columns = chunks[number]
+        order = order_of(number)
+        bit = order[stage]
+        arriving[number].wait_recv()
+        left = [b for b in every if b not in order[:stage]]
+        spot = place(left, {bit: 1 - me[bit]}, columns)
+        buffer = held[stage - 1][index]
+        buffer[spot] = summed(number, stage, {bit: 1 - me[bit]}).astype(buffer.dtype)
+        left.remove(bit)
+        target = held[stage][index].at[place(left, {}, columns)]
+        arriving[number] = send(buffer.at[spot], target, stage, number, bit)
+
+    def settle(number):
+        index, columns = chunks[number]
         arriving[number].wait_recv()
         total = summed(number, bits, {})
-        if not gather:
+        if not gathers[index]:
             outs[index][:, columns] = total
-            continue
+            return
+        spot = place(every, me, columns)
+        whole[index][spot] = total.astype(whole[index].dtype)
+        target = whole[index].at[spot]
+        arriving[number] = send(target, target, bits, number, order_of(number)[-1])
+
+    def double(number, back):
+        index, columns = chunks[number]
+        if not gathers[index]:
+            return
         order = order_of(number)
-        spot = place(every, me, columns)
-        whole[index][spot] = total.astype(LOW)
-        target = whole[index].at[spot]
-        arriving[number] = send(target, target, bits, number, order[-1])
-
-    if gather:
-        for back in range(1, bits):
-            for number, (index, columns) in enumerate(chunks):
-                order = order_of(number)
-                arriving[number].wait_recv()
-                known = {bit: me[bit] for bit in order[: bits - back]}
-                target = whole[index].at[place(every, known, columns)]
-                arriving[number] = send(target, target, bits + back, number, order[bits - back - 1])
-        for number in range(len(chunks)):
-            arriving[number].wait_recv()
-        for copy in copies:
-            copy.wait_send()
-        locals_ = [
-            pltpu.make_async_copy(whole[index], outs[index], out_sem.at[index])
-            for index in range(count)
+        arriving[number].wait_recv()
+        if back == bits:
+            return
+        known = {bit: me[bit] for bit in order[: bits - back]}
+        target = whole[index].at[place(every, known, columns)]
+        arriving[number] = send(target, target, bits + back, number, order[bits - back - 1])
+
+    numbers = range(len(chunks))
+    work = [functools.partial(halve, n, stage) for stage in range(1, bits) for n in numbers]
+    work += [functools.partial(settle, n) for n in numbers]
+    if any(gathers):
+        work += [functools.partial(double, n, back) for back in range(1, bits + 1) for n in numbers]
+
+    for number in numbers:
+        halve_first(number)
+    if sums:
+        zacc, zsum, up_send, up_recv, back_send, back_recv, keep_sem = refs[3:]
+        last = lanes - 1
+        step = zin[0].shape[0] // pieces
+        near = (2 * spot_z) // lanes
+        far = 1 - near
+
+        def chain(flow, piece):
+            spot = spot_z + flow * (last - 2 * spot_z)
+            ahead = {"tensor": (spot_z + lanes + 1 - 2 * flow) % lanes}
+            behind = {"tensor": (spot_z + lanes - 1 + 2 * flow) % lanes}
+            rows = pl.ds(piece * step, step)
+
+            def up(source):
+                return pltpu.make_async_remote_copy(
+                    src_ref=source,
+                    dst_ref=zacc.at[flow, rows],
+                    send_sem=up_send.at[flow, piece],
+                    recv_sem=up_recv.at[flow, piece],
+                    device_id=ahead,
+                    device_id_type=mesh_ids,
+                )
+
+            def back():
+                return pltpu.make_async_remote_copy(
+                    src_ref=zsum.at[flow, rows],
+                    dst_ref=zsum.at[flow, rows],
+                    send_sem=back_send.at[flow, piece],
+                    recv_sem=back_recv.at[flow, piece],
+                    device_id=behind,
+                    device_id_type=mesh_ids,
+                )
+
+            return spot, rows, up, back
+
+        def begin(flow, piece):
+            spot, rows, up, back = chain(flow, piece)
+
+            @pl.when(spot == 0)
+            def _():
+                up(zin[flow].at[rows]).start()
+
+        def climb(flow, piece):
+            spot, rows, up, back = chain(flow, piece)
+
+            @pl.when(spot > 0)
+            def _():
+                up(zacc.at[flow, rows]).wait_recv()
+                own = jnp.where(flow == 0, zin[0][rows, :].astype(F32), zin[1][rows, :].astype(F32))
+                total = (own + zacc[flow, rows, :].astype(F32)).astype(LOW)
+
+                @pl.when(spot < last)
+                def _():
+                    zacc[flow, rows, :] = total
+                    up(zacc.at[flow, rows]).start()
+
+                @pl.when(spot == last)
+                def _():
+                    zsum[flow, rows, :] = total
+                    back().start()
+
+        def descend(flow, piece):
+            spot, rows, up, back = chain(flow, piece)
+
+            @pl.when(spot < last)
+            def _():
+                back().wait_recv()
+
+                @pl.when(spot > 0)
+                def _():
+                    back().start()
+
+        def close(flow, piece):
+            spot, rows, up, back = chain(flow, piece)
+
+            @pl.when(spot < last)
+            def _():
+                up(zacc.at[flow, rows]).wait_send()
+
+            @pl.when(spot > 0)
+            def _():
+                back().wait_send()
+
+        for piece in range(pieces):
+            for flow in range(2):
+                begin(flow, piece)
+        steps = []
+        for work_of, first, second in ((climb, near, far), (descend, far, near)):
+            for piece in range(pieces + lag):
+                if piece < pieces:
+                    steps.append(functools.partial(work_of, first, piece))
+                if piece >= lag:
+                    steps.append(functools.partial(work_of, second, piece - lag))
+        done = 0
+        for number, one in enumerate(steps):
+            one()
+            due = len(work) * max(0, number + 1 - len(steps) // 8) // (len(steps) - len(steps) // 8)
+            for other in work[done:due]:
+                other()
+            done = due
+        for piece in range(pieces):
+            for flow in range(2):
+                close(flow, piece)
+    else:
+        for one in work:
+            one()
+    for copy in copies:
+        copy.wait_send()
+    locals_ = [
+        pltpu.make_async_copy(whole[index], outs[index], out_sem.at[index])
+        for index in range(count)
+        if gathers[index]
+    ]
+    if sums:
+        locals_ += [
+            pltpu.make_async_copy(zsum.at[flow], zout[flow], keep_sem.at[flow]) for flow in range(2)
         ]
-        for copy in locals_:
-            copy.start()
-        for copy in locals_:
-            copy.wait()
-    else:
-        for copy in copies:
-            copy.wait_send()
-
-
-def exchange(arrays, sizes, name, number, gather=False, chunk=512):
+    for copy in locals_:
+        copy.start()
+    for copy in locals_:
+        copy.wait()
+
+
+def exchange(arrays, gathers, sizes, name, number, partials=(), lanes=1, chunk=512, pieces=16, lag=2):
     seq_bits, bits = owner_bits(*sizes)
     parts = 2**bits
     views, chunks = [], []
@@ -209,28 +339,37 @@
             chunks.append((index, pl.ds(begin, step)))
     count = len(arrays)
     shapes = [view.shape[bits:] for view in views]
+    kinds = [view.dtype for view in views]
     scratch = [
-        pltpu.VMEM((2,) * (bits - 1 - stage) + shape, LOW) for stage in range(bits) for shape in shapes
+        pltpu.VMEM((2,) * (bits - 1 - stage) + shape, kind)
+        for stage in range(bits)
+        for shape, kind in zip(shapes, kinds)
     ]
-    slots = bits
-    if gather:
-        scratch += [pltpu.VMEM((2,) * bits + shape, LOW) for shape in shapes]
-        slots = 2 * bits
-        out_shape = [jax.ShapeDtypeStruct((2,) * bits + shape, LOW) for shape in shapes]
-        out_specs = [pl.BlockSpec(memory_space=pl.ANY)] * count
-    else:
-        out_shape = [jax.ShapeDtypeStruct(shape, F32) for shape in shapes]
-        out_specs = [pl.BlockSpec(memory_space=pltpu.VMEM)] * count
+    out_shape, out_specs = [], []
+    for shape, kind, gather in zip(shapes, kinds, gathers):
+        everywhere = (2,) * bits + shape
+        scratch.append(pltpu.VMEM(everywhere if gather else (8, 128), kind))
+        out_shape.append(jax.ShapeDtypeStruct(everywhere if gather else shape, kind if gather else F32))
+        out_specs.append(pl.BlockSpec(memory_space=pl.ANY if gather else pltpu.VMEM))
+    slots = (2 * bits if any(gathers) else bits, len(chunks))
     scratch += [
-        pltpu.SemaphoreType.DMA((slots, len(chunks))),
-        pltpu.SemaphoreType.DMA((slots, len(chunks))),
+        pltpu.SemaphoreType.DMA(slots),
+        pltpu.SemaphoreType.DMA(slots),
         pltpu.SemaphoreType.DMA((count,)),
     ]
+    if partials:
+        scratch += [pltpu.VMEM((2,) + partials[0].shape, partials[0].dtype)] * 2
+        scratch += [pltpu.SemaphoreType.DMA((2, pieces)) for _ in range(4)]
+        scratch.append(pltpu.SemaphoreType.DMA((2,)))
+        out_shape += [jax.ShapeDtypeStruct(p.shape, p.dtype) for p in partials]
+        out_specs += [pl.BlockSpec(memory_space=pl.ANY)] * 2
     moved = sum(view.size for view in views) * 2
     results = pl.pallas_call(
-        functools.partial(exchange_kernel, count, bits, seq_bits, chunks, gather),
+        functools.partial(
+            exchange_kernel, gathers, bits, seq_bits, chunks, lanes, pieces if partials else 0, lag
+        ),
         out_shape=out_shape,
-        in_specs=[pl.BlockSpec(memory_space=pltpu.VMEM)] * count,
+        in_specs=[pl.BlockSpec(memory_space=pltpu.VMEM)] * (count + len(partials)),
         out_specs=out_specs,
         scratch_shapes=scratch,
         compiler_params=pltpu.CompilerParams(
@@ -238,10 +377,11 @@
         ),
         cost_estimate=pl.CostEstimate(flops=0, bytes_accessed=16 * moved, transcendentals=0),
         name=name,
-    )(*views)
-    if gather:
-        results = [r.reshape(a.shape) for r, a in zip(results, arrays)]
-    return results
+    )(*views, *partials)
+    sums = [
+        r.reshape(a.shape) if gather else r for r, a, gather in zip(results, arrays, gathers)
+    ]
+    return sums, list(results[count:])
 
 
 def schulz_kernel(packed, tile, gram_ref, moment_ref, step_ref, gram, low_gram, poly, low_poly, low_mix):
@@ -408,16 +548,11 @@
             return grads[:tokens] + other.astype(F32)
         return lax.psum_scatter(grads, "seq", scatter_dimension=0, tiled=True)
 
-    queue = []
-
-    def tensor_sum(partial):
-        if queue:
-            partial, queue[0] = lax.optimization_barrier((partial, queue[0]))
-        total = lax.psum(partial, "tensor")
-        queue[:] = [total]
-        return total
-
     w_output_all = lax.all_gather(w_output, "tensor", axis=0, tiled=True)
+    lanes = lax.axis_size("tensor")
+
+    def after(value, earlier):
+        return lax.optimization_barrier((value, earlier))[0]
 
     def stage_one(b):
         s = {}
@@ -464,7 +599,9 @@
             .reshape(tokens, q_width)
             .astype(LOW)
         )
-        s["mixed_all"] = lax.all_gather(s["mixed"], "tensor", axis=1, tiled=True)
+        s["mixed_all"] = lax.all_gather(
+            after(s["mixed"], w_output_all), "tensor", axis=1, tiled=True
+        )
 
     def stage_three(s, b):
         middle = s["resid"] + dot(s["mixed_all"], w_output_all)
@@ -481,7 +618,8 @@
         s["gate_grad"] = (inner_grad * up_value * sigma * (1.0 + gate * (1.0 - sigma))).astype(LOW)
         s["up_grad"] = (inner_grad * active).astype(LOW)
         two_partial = dot_nt(s["gate_grad"], w_gate) + dot_nt(s["up_grad"], w_up)
-        s["two_sum"] = tensor_sum(two_partial.astype(LOW))
+        s["two_partial"] = two_partial.astype(LOW)
+        s["ffn_partial"] = dot(s["inner"], w_down).astype(LOW)
         s["middle"] = middle
 
     def stage_four(s, b):
@@ -528,8 +666,7 @@
             + dot_nt(s["key_low"], key_weight)
             + dot_nt(s["value_low"], value_weight)
         )
-        s["ffn_sum"] = tensor_sum(dot(s["inner"], w_down).astype(LOW))
-        s["one_sum"] = tensor_sum(one_partial.astype(LOW))
+        s["one_partial"] = one_partial.astype(LOW)
 
     def stage_five(s):
         normed_one_grad = s["one_sum"].astype(F32)
@@ -550,10 +687,8 @@
 
     sizes = (seq_size, inputs_share)
 
-    def finish(grads, olds, name, number):
-        sums = exchange(grads, sizes, name + "_grads", number)
-        moments = [MU_MUON * old + total for old, total in zip(olds, sums)]
-        return sums, moments
+    def momenta(olds, sums):
+        return [MU_MUON * old + total for old, total in zip(olds, sums)]
 
     def gram_of(moment):
         low = moment.astype(LOW)
@@ -564,6 +699,9 @@
         half = low.shape[1] // 2
         front, back = low[:, :half], low[:, half:]
         return [dot_tn(front, front), dot_tn(front, back), dot_tn(back, back)]
+
+    def tensor_pair(name):
+        return [states[0][name], states[1][name]]
 
     states = [stage_one(b) for b in range(batches)]
     for s in states:
@@ -576,43 +714,64 @@
         weight_grad(column("normed_two"), column("up_grad")),
         weight_grad(cots, column("inner")),
     ]
-    for b, s in enumerate(states):
-        stage_four(s, b)
-    ffn_sums, ffn_moments = finish(ffn_grads, [mom_gate, mom_up, mom_down.T], "ffn", 0)
+    ffn_sums, two_sums = exchange(
+        ffn_grads, [False] * 3, sizes, "ffn_grads", 0, tensor_pair("two_partial"), lanes
+    )
+    for s, total in zip(states, two_sums):
+        s["two_sum"] = total
+    states[0]["ffn_sum"] = lax.psum(after(states[0]["ffn_partial"], two_sums[0]), "tensor")
+    ffn_moments = momenta([mom_gate, mom_up, mom_down.T], ffn_sums)
     half = ffn_moments[0].shape[1] // 2
     grams = jnp.concatenate(
         [jnp.concatenate(packed_gram(m), axis=0).astype(LOW) for m in ffn_moments], axis=1
     )
-    (grams,) = exchange([grams], sizes, "ffn_grams", 1, gather=True)
-    ffn_steps = [
-        newton_schulz(
-            grams[:, i * half : (i + 1) * half].reshape(3, half, half), ffn_moments[i], True
-        )
-        for i in range(3)
-    ]
+    for b, s in enumerate(states):
+        stage_four(s, b)
     attn_grads = [
         weight_grad(column("normed_one"), column("query_low")),
         weight_grad(column("normed_one"), column("key_low")),
         weight_grad(column("normed_one"), column("value_low")),
         weight_grad(column("middle_low"), column("mixed")),
     ]
+    attn_sums, one_sums = exchange(
+        [grams] + attn_grads,
+        [True] + [False] * 4,
+        sizes,
+        "attn_grads",
+        1,
+        tensor_pair("one_partial"),
+        lanes,
+    )
+    grams, attn_sums = attn_sums[0], attn_sums[1:]
+    for s, total in zip(states, one_sums):
+        s["one_sum"] = total
+    states[1]["ffn_sum"] = lax.psum(
+        after(states[1]["ffn_partial"], (states[0]["ffn_sum"], one_sums[0])), "tensor"
+    )
     for s in states:
         stage_five(s)
-    attn_sums, attn_moments = finish(
-        attn_grads, [mom_query, key_momentum, value_momentum, mom_output.T], "attn", 2
-    )
+    ffn_steps = [
+        newton_schulz(
+            grams[:, i * half : (i + 1) * half].reshape(3, half, half), ffn_moments[i], True
+        )
+        for i in range(3)
+    ]
+    attn_moments = momenta([mom_query, key_momentum, value_momentum, mom_output.T], attn_sums)
     pair = jnp.concatenate([gram_of(attn_moments[1]), gram_of(attn_moments[2])], axis=1)
     grams = jnp.concatenate([gram_of(attn_moments[0]), gram_of(attn_moments[3]), pair], axis=0)
-    (grams,) = exchange([grams], sizes, "attn_grams", 3, gather=True)
+    gains = jnp.stack([sum(column("gain_one")), sum(column("gain_two"))])
+    owners = seq_size * inputs_share
+    (grams, gains), _ = exchange(
+        [grams, gains.reshape(owners, -1)], [True, True], sizes, "attn_grams", 2
+    )
+    gains = gains.reshape(2, -1)
+    attn_total, ffn_total = gains[0], gains[1]
     attn_steps = [
         newton_schulz(grams[:q_width], attn_moments[0], False),
         newton_schulz(grams[2 * q_width :, :kv_width], attn_moments[1], False),
         newton_schulz(grams[2 * q_width :, kv_width:], attn_moments[2], False),
         newton_schulz(grams[q_width : 2 * q_width], attn_moments[3], False),
     ]
-    gains = jnp.stack([sum(column("gain_one")), sum(column("gain_two"))])
-    gains = lax.psum(gains, ("dp", "seq"))
-    attn_total, ffn_total = gains[0], gains[1]
     outputs = jnp.stack(column("block_out"))
     input_grads = jnp.stack(column("input_grad"))
     attn_one, attn_two, attn_step = adam(attn_total, attn_first, attn_second)

time: 940 us -> 765 us (0.81)
  waiting for transfers between devices: 385 us -> 171 us
  Pallas kernels: 242 us -> 303 us
  blocking collectives: 23.9 us -> 0 us
    psum x6 -> x2, waiting for transfers between devices: 242 us -> 57.5 us  [the longest x1 57.5 us: shards(): lax.psum(after(states[0]['ffn_partial'], two_sums[0]), 'tensor')]
    pallas_call x4 -> x3, Pallas kernels: 148 us -> 208 us  [exchange(): pl.pallas_call(functools.partial(exchange_kernel, gathers, bits, seq_bits...]
    all_gather x1, waiting for transfers between devices: 89.9 us -> 49.4 us  [shards(): w_output_all = lax.all_gather(w_output, 'tensor', axis=0, tiled=True)]
    psum x1 -> x0, blocking collectives: 23.9 us -> none  [shards(): gains = lax.psum(gains, ('dp', 'seq'))]
    all_gather x2, waiting for transfers between devices: 38.6 us -> 54.2 us  [stage_two(): lax.all_gather(after(s['mixed'], w_output_all), 'tensor', axis=1, tiled=T...]
    unnamed x264 -> x300, local copies, waits for them, and re-layouts: 27.2 us -> 21.8 us
  transfers between devices with their start and end apart: 13 -> 9, of which waited for: 12 -> 6; matrix products, arithmetic and copies ran while one was open for 8% -> 10% of each run, Pallas kernels for 15% -> 12%
where the time goes in v2:
time: 765 us; the launch traced here: 759 us
  Pallas kernels  303 us (40%)
  waiting for transfers between devices  171 us (22%)
  matrix products  155 us (20%)
  other arithmetic  64.2 us (8%)
  local copies, waits for them, and re-layouts  44.9 us (6%)
  between operations  16.1 us (2%)
    pallas_call x3, Pallas kernels, exchange(): pl.pallas_call(functools.partial(exchange_kernel, gathers, bits, seq_bits...  208 us
    pallas_call x7, Pallas kernels, newton_schulz(): pl.pallas_call(functools.partial(schulz_kernel, packed, tile), out_shape=...  94.3 us
    psum x1, waiting for transfers between devices, shards(): lax.psum(after(states[0]['ffn_partial'], two_sums[0]), 'tensor')  57.5 us
    all_gather x2, waiting for transfers between devices, stage_two(): lax.all_gather(after(s['mixed'], w_output_all), 'tensor', axis=1, tiled=T...  54.2 us
    dot_general x27, matrix products, dot_tn(): lax.dot_general(left, right, (((0,), (0,)), ((), ())), preferred_element_...  50.9 us
    all_gather x1, waiting for transfers between devices, shards(): w_output_all = lax.all_gather(w_output, 'tensor', axis=0, tiled=True)  49.4 us
    dot_general x16, matrix products, dot_nt(): lax.dot_general(left, right, (((1,), (1,)), ((), ())), preferred_element_...  38.5 us
    dot_general x14, matrix products, dot(): return jnp.dot(left, right, preferred_element_type=F32)  36.7 us
  transfers between devices with their start and end apart: 9, of which 6 were waited for; matrix products, arithmetic and copies ran while one was open for 10% of the time, Pallas kernels for 12%

profile of v2, /device:TPU:0, one launch (start us, length us, event | category | flops | bytes accessed | tf_op | source)
XLA Modules:
  0.0 759.5 jit_solution(4641155710252912314)
XLA Ops:
  13.2 2.7 fusion.56
  20.2 3.0 collective-permute-start
  25.7 2.6 copy.90
  28.3 2.8 fusion.88
  33.8 2.4 copy.89
  36.2 2.3 copy.93
  39.7 1.9 pad_maximum_fusion.11
  42.8 2.0 pad_maximum_fusion.7
  47.8 2.2 copy-done.31
  50.0 2.3 fusion.99
  52.3 49.4 %all-gather.4.cloned.1.call-done = bf16[1536,1536]{1,0:T(8,128)(2,1)} async-done(((bf16[384,1536]{1,0:T(8,128)(2,1)}), bf16[1536,1536]{1,0:T(8,128)(2,1)}) %all-gather.4.cloned.1.call-update) | async-done | bytes 4718608 | tf_op jit(solution)/shard_map/all_gather | solution.py:551
  103.0 3.1 fusion.196
  107.3 2.1 copy-done.32
  109.4 2.3 fusion.98
  113.7 25.1 %all-gather.6.cloned.1.call-done = bf16[512,1536]{0,1:T(8,128)(2,1)} async-done(((bf16[512,384]{0,1:T(8,128)(2,1)}), bf16[512,1536]{0,1:T(8,128)(2,1)}) %all-gather.6.cloned.1.call-update) | async-done | bytes 1572880 | tf_op jit(solution)/shard_map/all_gather | solution.py:602
  138.8 7.8 %multiply_reduce_fusion.1 = (f32[512]{0:T(512)S(1)}, f32[512,1536]{1,0:T(8,128)}) fusion(bf16[512,1536]{0,1:T(8,128)(2,1)} %all-gather.6.cloned.1.call-done, bf16[1536,1536]{1,0:T(8,128)(2,1)} %all-gather.4.cloned.1.call-done, bf16[1,2,512,1536]{3,2,1,0:T(8,128)(2,1)} %param.24), kind=kOutput, calls=%fused_computation.102 | convolution fusion | flops 2419064320 | bytes 11012096 | tf_op jit(solution)/shard_map/dot_general | solution.py:63
  147.2 29.1 %all-gather.8.cloned.1.call-done = bf16[512,1536]{0,1:T(8,128)(2,1)} async-done(((bf16[512,384]{0,1:T(8,128)(2,1)}), bf16[512,1536]{0,1:T(8,128)(2,1)}) %all-gather.8.cloned.1.call-update) | async-done | bytes 1572880 | tf_op jit(solution)/shard_map/all_gather | solution.py:602
  176.3 6.4 multiply_reduce_fusion
  184.4 2.2 copy-done.131
  186.6 3.1 fusion.201
  189.7 3.2 fusion.202
  196.6 3.6 multiply_convert_fusion.4
  200.2 3.7 fusion.204
  203.9 4.6 fusion.200
  208.4 4.5 fusion.84
  212.9 2.9 convolution_convert_fusion.1
  215.8 6.3 multiply_convert_fusion.3
  222.2 3.6 fusion.205
  225.8 4.6 fusion.203
  230.3 3.1 fusion.65.refs_3_
  233.4 4.1 fusion.38
  237.5 4.7 copy.95
  242.2 6.3 fusion.66.refs_4_
  248.5 6.4 add_convert_fusion.1
  255.0 3.5 add_convert_fusion.2
  258.5 86.5 %ffn_grads.1 = (f32[192,1024]{1,0:T(8,128)S(1)}, f32[192,1024]{1,0:T(8,128)S(1)}, f32[192,1024]{1,0:T(8,128)S(1)}, bf16[512,1536]{1,0:T(8,128)(2,1)S(1)}, bf16[512,1536]{1,0:T(8,128)(2,1)S(1)}) custom-call(bf16[2,2,2,192,1024]{4,3,2,1,0:T(8,128)(2,1)} %bitcast.367, bf16[2,2,2,192,1024]{4,3,2,1,0:T(8,128)(2,1)} %bitcast.366, ...), custom_call_target="tpu_custom_call" | custom-call | bytes 150994944 | tf_op jit(solution)/shard_map/ffn_grads/pallas_call | solution.py:367
  359.0 2.6 fusion.52
  367.7 2.4 pad_maximum_fusion.refs_0_
  370.1 2.9 convolution_convert_fusion
  373.0 57.5 %all-reduce.3.cloned.1.call-done = bf16[512,1536]{1,0:T(8,128)(2,1)} async-done(((bf16[512,1536]{1,0:T(8,128)(2,1)}), bf16[512,1536]{1,0:T(8,128)(2,1)}) %all-reduce.3.cloned.1.call-update) | async-done | bytes 1572880 | tf_op jit(solution)/shard_map/psum | solution.py:722
  430.5 7.6 %fusion.47 = (f32[512,1536]{1,0:T(8,128)S(1)}, f32[512,1536]{1,0:T(8,128)S(1)}, f32[1,512,1536]{2,1,0:T(8,128)}) fusion(bf16[512,1536]{1,0:T(8,128)(2,1)} %copy-done.3, f32[512,1536]{1,0:T(8,128)} %copy-done.33, f32[512]{0:T(512)} %broadcast_multiply_fusion.2, f32[512]{0:T(512)} %copy-done.112, f32[1536]{0:T(1024)} %param.35, ...), kind=kLoop, calls=%fused_computation.79 | loop fusion | flops 14155776 | bytes 23607296 | tf_op jit(solution)/shard_map/add | solution.py:628
  439.0 6.2 fusion.10
  445.3 5.3 fusion
  450.7 2.4 fusion.2
  460.3 2.8 fusion.5
  475.7 6.2 collective-permute-done.3
  485.7 2.8 collective-permute-done.2
  494.4 2.4 copy.103
  496.7 3.2 fusion.71
  502.5 99.7 %attn_grads.1 = (bf16[2,2,2,192,1536]{4,3,2,1,0:T(8,128)(2,1)}, f32[192,384]{1,0:T(8,128)S(1)}, f32[192,192]{1,0:T(8,128)S(1)}, f32[192,192]{1,0:T(8,128)S(1)}, ...) custom-call(bf16[2,2,2,192,1536]{4,3,2,1,0:T(8,128)(2,1)} %pad_maximum_fusion.refs_0_, ...), custom_call_target="tpu_custom_call" | custom-call | bytes 132120576 | tf_op jit(solution)/shard_map/attn_grads/pallas_call | solution.py:367
  602.2 3.8 fusion.55
  610.5 22.1 %attn_grams.1 = (bf16[2,2,2,120,384]{4,3,2,1,0:T(8,128)(2,1)S(1)}, f32[2,2,2,1,384]{4,3,2,1,0:T(1,128)S(1)}) custom-call(bf16[2,2,2,120,384]{4,3,2,1,0:T(8,128)(2,1)S(1)} %bitcast.333, f32[2,2,2,1,384]{4,3,2,1,0:T(1,128)S(1)} %pad_maximum_fusion.14.refs_1_), custom_call_target="tpu_custom_call" | custom-call | bytes 11894784 | tf_op jit(solution)/shard_map/attn_grams/pallas_call | solution.py:367
  633.5 4.7 fusion.181
  638.2 6.5 schulz.10
  646.3 25.4 %schulz.13 = f32[192,1024]{1,0:T(8,128)} custom-call(bf16[3,512,512]{2,1,0:T(8,128)(2,1)S(1)} %bitcast.336, f32[192,1024]{1,0:T(8,128)S(1)} %copy-done.29), custom_call_target="tpu_custom_call" | custom-call | flops 16240345088 | bytes 3145728 | tf_op jit(solution)/shard_map/schulz/pallas_call | solution.py:465
  671.7 25.6 %schulz.12 = f32[192,1024]{1,0:T(8,128)} custom-call(bf16[3,512,512]{2,1,0:T(8,128)(2,1)S(1)} %bitcast.335, f32[192,1024]{1,0:T(8,128)S(1)} %copy-done.28), custom_call_target="tpu_custom_call" | custom-call | flops 16240345088 | bytes 3145728 | tf_op jit(solution)/shard_map/schulz/pallas_call | solution.py:465
  697.3 1.9 fusion.44
  699.3 3.2 maximum_bitcast_fusion.1
  703.7 6.5 schulz.7
  710.2 2.4 schulz.9
  712.6 2.4 schulz.8
  715.0 25.6 %schulz.11 = f32[192,1024]{1,0:T(8,128)} custom-call(bf16[3,512,512]{2,1,0:T(8,128)(2,1)S(1)} %bitcast.334, f32[192,1024]{1,0:T(8,128)S(1)} %copy-done.27), custom_call_target="tpu_custom_call" | custom-call | flops 16240345088 | bytes 3145728 | tf_op jit(solution)/shard_map/schulz/pallas_call | solution.py:465
  740.6 2.9 add_bitcast_fusion
  743.9 3.1 maximum_bitcast_fusion
  (433 shorter events, 96.9 us)
Async XLA Ops:
  7.2 189.4 %copy-start = (bf16[1024,1536]{1,0:T(8,128)(2,1)S(1)}, bf16[1024,1536]{1,0:T(8,128)(2,1)}, u32[]{:S(2)}) copy-start(bf16[1024,1536]{1,0:T(8,128)(2,1)} %param.33) | copy-start | bytes 9437188
  7.2 94.5 %all-gather.4.cloned.1.call-start = ((), (), s32[]{:S(2)}) async-start(), calls=%async_computation | async-start | bytes 5898240 | tf_op jit(solution)/shard_map/all_gather | solution.py:551
  8.0 130.8 %all-gather.6.cloned.1.call-start = ((), (), s32[]{:S(2)}) async-start(), calls=%async_computation.1 | async-start | bytes 1966080 | tf_op jit(solution)/shard_map/all_gather | solution.py:602
  15.9 12.4 %copy-start.122 = (f32[512]{0:T(512)}, f32[512]{0:T(512)S(1)}, u32[]{:S(2)}) copy-start(f32[512]{0:T(512)S(1)} %get-tuple-element.173) | copy-start | bytes 6148
  15.9 16.1 %copy-start.120 = (f32[512]{0:T(512)}, f32[512]{0:T(512)S(1)}, u32[]{:S(2)}) copy-start(f32[512]{0:T(512)S(1)} %get-tuple-element.172) | copy-start | bytes 6148
  17.4 6.6 copy-start.87
  17.4 13.7 %copy-start.53 = (f32[512,48]{0,1:T(8,128)}, f32[512,48]{0,1:T(8,128)S(1)}, u32[]{:S(2)}) copy-start(f32[512,48]{0,1:T(8,128)S(1)} %get-tuple-element.153) | copy-start | bytes 294916
  17.4 15.5 %copy-start.55 = (f32[512,48]{0,1:T(8,128)}, f32[512,48]{0,1:T(8,128)S(1)}, u32[]{:S(2)}) copy-start(f32[512,48]{0,1:T(8,128)S(1)} %get-tuple-element.148) | copy-start | bytes 294916
  20.2 21.4 %collective-permute-start = (bf16[512,384]{0,1:T(8,128)(2,1)}, bf16[512,384]{0,1:T(8,128)(2,1)}, u32[]{:S(2)}, u32[]{:S(2)}) collective-permute-start(bf16[512,384]{0,1:T(8,128)(2,1)} %pad_maximum_fusion.8), channel_id=1, source_target_pairs={{0,4},{4,0},{1,5},{5,1},{2,6},{6,2},{3,7},{7,3},{8,12},{12,8},{9,1... | collective-permute-start | bytes 1179656 | tf_op jit(solution)/shard_map/ppermute | solution.py:542
  25.7 17.1 %collective-permute-start.1 = (bf16[512,384]{0,1:T(8,128)(2,1)}, bf16[512,384]{0,1:T(8,128)(2,1)}, u32[]{:S(2)}, u32[]{:S(2)}) collective-permute-start(bf16[512,384]{0,1:T(8,128)(2,1)} %pad_maximum_fusion.10), channel_id=1, source_target_pairs={{0,4},{4,0},{1,5},{5,1},{2,6},{6,2},{3,7},{7,3},{8,12},{12,8},{9,1... | collective-permute-start | bytes 1179656 | tf_op jit(solution)/shard_map/ppermute | solution.py:542
  33.8 9.0 %copy-start.64 = (bf16[512,2,96]{0,2,1:T(8,128)(2,1)S(1)}, bf16[512,2,96]{0,2,1:T(8,128)(2,1)}, u32[]{:S(2)}) copy-start(bf16[512,2,96]{0,2,1:T(8,128)(2,1)} %copy-done.63) | copy-start | bytes 589828
  38.5 6.3 copy-start.97
  39.6 6.9 copy-start.71
  50.0 53.0 %copy-start.73 = (bf16[512,4,96]{0,2,1:T(8,128)(2,1)S(1)}, bf16[512,4,96]{0,2,1:T(8,128)(2,1)}, u32[]{:S(2)}) copy-start(bf16[512,4,96]{0,2,1:T(8,128)(2,1)} %pad_maximum_fusion.11) | copy-start | bytes 1179652
  101.8 74.5 %all-gather.8.cloned.1.call-start = ((), (), s32[]{:S(2)}) async-start(), calls=%async_computation.2 | async-start | bytes 1966080 | tf_op jit(solution)/shard_map/all_gather | solution.py:602
  111.8 318.8 %all-reduce.3.cloned.1.call-start = ((), (), s32[]{:S(2)}) async-start(), calls=%async_computation.3 | async-start | bytes 3145728 | tf_op jit(solution)/shard_map/psum | solution.py:722
  176.3 6.4 copy-start.39
  176.3 6.4 copy-start.106
  176.3 6.4 copy-start.110
  184.4 19.5 %copy-start.67 = (bf16[512,1536]{1,0:T(8,128)(2,1)}, bf16[512,1536]{1,0:T(8,128)(2,1)S(1)}, u32[]{:S(2)}) copy-start(bf16[512,1536]{1,0:T(8,128)(2,1)S(1)} %get-tuple-element.137) | copy-start | bytes 4718596
  215.8 6.3 copy-start.130
  222.1 11.3 %copy-start.83 = (bf16[512,1024]{1,0:T(8,128)(2,1)}, bf16[512,1024]{1,0:T(8,128)(2,1)S(1)}, u32[]{:S(2)}) copy-start(bf16[512,1024]{1,0:T(8,128)(2,1)S(1)} %get-tuple-element.98) | copy-start | bytes 3145732
  222.1 8.2 %copy-start.137 = (f32[512,1536]{1,0:T(8,128)S(1)}, f32[512,1536]{1,0:T(8,128)}, u32[]{:S(2)}) copy-start(f32[512,1536]{1,0:T(8,128)} %fusion.204) | copy-start | bytes 9437188
  225.7 7.7 %slice-start.4 = ((s8[6291456]{0:T(1024)(128)(4,1)}), s8[4194304]{0:T(1024)(128)(4,1)S(1)}, s32[]{:S(2)}) async-start(s8[6291456]{0:T(1024)(128)(4,1)} %bitcast.356), calls=%async_computation.9 | async-start | bytes 8388608
  242.2 6.3 copy-start.66
  242.2 6.3 copy-start.136
  242.2 12.8 %slice-start.6 = ((s8[6291456]{0:T(1024)(128)(4,1)}), s8[4194304]{0:T(1024)(128)(4,1)S(1)}, s32[]{:S(2)}) async-start(s8[6291456]{0:T(1024)(128)(4,1)} %bitcast.408), calls=%async_computation.11 | async-start | bytes 8388608
  248.5 6.5 slice-start.7
  248.5 6.5 copy-start.135
  258.5 86.5 %copy-start.94 = (f32[192,1024]{1,0:T(8,128)S(1)}, f32[192,1024]{1,0:T(8,128)}, u32[]{:S(2)}) copy-start(f32[192,1024]{1,0:T(8,128)} %param.41) | copy-start | bytes 2359300
  345.0 6.2 copy-start.7
  345.0 6.2 copy-start.9
  345.0 9.6 %copy-start.5 = (f32[192,1024]{1,0:T(8,128)}, f32[192,1024]{1,0:T(8,128)S(1)}, u32[]{:S(2)}) copy-start(f32[192,1024]{1,0:T(8,128)S(1)} %get-tuple-element.55) | copy-start | bytes 2359300
  345.0 14.0 %copy-start.2 = (bf16[512,1536]{1,0:T(8,128)(2,1)}, bf16[512,1536]{1,0:T(8,128)(2,1)S(1)}, u32[]{:S(2)}) copy-start(bf16[512,1536]{1,0:T(8,128)(2,1)S(1)} %get-tuple-element.51) | copy-start | bytes 4718596
  345.0 14.0 %copy-start.3 = (bf16[512,1536]{1,0:T(8,128)(2,1)}, bf16[512,1536]{1,0:T(8,128)(2,1)S(1)}, u32[]{:S(2)}) copy-start(bf16[512,1536]{1,0:T(8,128)(2,1)S(1)} %get-tuple-element.56) | copy-start | bytes 4718596
  352.3 6.7 copy-start.40
  362.2 378.4 %all-reduce.5.cloned.1.call-start = ((), (), s32[]{:S(2)}) async-start(), calls=%async_computation.4 | async-start | bytes 3145728 | tf_op jit(solution)/shard_map/psum | solution.py:748
  430.5 7.6 %copy-start.47 = (bf16[384,1536]{1,0:T(8,128)(2,1)S(1)}, bf16[384,1536]{1,0:T(8,128)(2,1)}, u32[]{:S(2)}) copy-start(bf16[384,1536]{1,0:T(8,128)(2,1)} %param.30) | copy-start | bytes 3538948
  438.2 27.2 %copy-start.37 = (f32[512,1536]{1,0:T(8,128)}, f32[512,1536]{1,0:T(8,128)S(1)}, u32[]{:S(2)}) copy-start(f32[512,1536]{1,0:T(8,128)S(1)} %get-tuple-element.105) | copy-start | bytes 9437188
  438.2 36.4 %copy-start.35 = (f32[512,1536]{1,0:T(8,128)}, f32[512,1536]{1,0:T(8,128)S(1)}, u32[]{:S(2)}) copy-start(f32[512,1536]{1,0:T(8,128)S(1)} %get-tuple-element.104) | copy-start | bytes 9437188
  439.0 6.3 copy-start.81
  439.0 11.6 %slice-start.2 = ((s8[8388608]{0:T(1024)(128)(4,1)}), s8[4194304]{0:T(1024)(128)(4,1)S(1)}, s32[]{:S(2)}) async-start(s8[8388608]{0:T(1024)(128)(4,1)} %bitcast.345), calls=%async_computation.7 | async-start | bytes 8388608
  469.9 12.1 %collective-permute-start.3 = (bf16[512,384]{0,1:T(8,128)(2,1)S(1)}, bf16[512,384]{0,1:T(8,128)(2,1)S(1)}, u32[]{:S(2)}, u32[]{:S(2)}) collective-permute-start(bf16[512,384]{0,1:T(8,128)(2,1)S(1)} %fusion.112), channel_id=1, source_target_pairs={{0,4},{4,0},{1,5},{5,1},{2,6},{6,2},{3,7},{7,3},{8,12},{12,8},{9,1... | collective-permute-start | bytes 1179656 | tf_op jit(solution)/shard_map/ppermute | solution.py:547
  472.7 15.7 %collective-permute-start.2 = (bf16[512,384]{0,1:T(8,128)(2,1)S(1)}, bf16[512,384]{0,1:T(8,128)(2,1)S(1)}, u32[]{:S(2)}, u32[]{:S(2)}) collective-permute-start(bf16[512,384]{0,1:T(8,128)(2,1)S(1)} %fusion.113), channel_id=1, source_target_pairs={{0,4},{4,0},{1,5},{5,1},{2,6},{6,2},{3,7},{7,3},{8,12},{12,8},{9,1... | collective-permute-start | bytes 1179656 | tf_op jit(solution)/shard_map/ppermute | solution.py:547
  475.7 6.5 copy-start.58
  502.5 99.7 %copy-start.44 = (bf16[1,2,512,1536]{3,2,1,0:T(8,128)(2,1)S(1)}, bf16[1,2,512,1536]{3,2,1,0:T(8,128)(2,1)}, u32[]{:S(2)}) copy-start(bf16[1,2,512,1536]{3,2,1,0:T(8,128)(2,1)} %param.24) | copy-start | bytes 9437188
  602.2 6.6 copy-start.104
  607.2 31.0 %copy-start.14 = (f32[192,384]{1,0:T(8,128)}, f32[192,384]{1,0:T(8,128)S(1)}, u32[]{:S(2)}) copy-start(f32[192,384]{1,0:T(8,128)S(1)} %bitcast_add_fusion.1.moment_ref) | copy-start | bytes 884740
  608.5 95.2 %copy-start.15 = (f32[192,384]{1,0:T(8,128)}, f32[192,384]{1,0:T(8,128)S(1)}, u32[]{:S(2)}) copy-start(f32[192,384]{1,0:T(8,128)S(1)} %multiply_add_fusion.4.moment_ref) | copy-start | bytes 884740
  609.8 100.4 %copy-start.20 = (f32[192,192]{1,0:T(8,128)}, f32[192,192]{1,0:T(8,128)S(1)}, u32[]{:S(2)}) copy-start(f32[192,192]{1,0:T(8,128)S(1)} %multiply_add_fusion.5.moment_ref) | copy-start | bytes 442372
  610.1 102.5 %copy-start.21 = (f32[192,192]{1,0:T(8,128)}, f32[192,192]{1,0:T(8,128)S(1)}, u32[]{:S(2)}) copy-start(f32[192,192]{1,0:T(8,128)S(1)} %multiply_add_fusion.6.moment_ref) | copy-start | bytes 442372
  638.2 6.6 copy-start.29
  644.8 57.7 %copy-start.114 = (f32[1536]{0:T(1024)}, f32[1536]{0:T(1024)S(1)}, u32[]{:S(2)}) copy-start(f32[1536]{0:T(1024)S(1)} %squeeze.10) | copy-start | bytes 18436
  644.8 58.3 %copy-start.115 = (f32[1536]{0:T(1024)}, f32[1536]{0:T(1024)S(1)}, u32[]{:S(2)}) copy-start(f32[1536]{0:T(1024)S(1)} %squeeze.11) | copy-start | bytes 18436
  646.3 25.4 %copy-start.12 = (bf16[1536,512]{1,0:T(8,128)(2,1)S(1)}, bf16[1536,512]{1,0:T(8,128)(2,1)}, u32[]{:S(2)}) copy-start(bf16[1536,512]{1,0:T(8,128)(2,1)} %get-tuple-element.94) | copy-start | bytes 4718596
  646.3 25.4 %copy-start.28 = (f32[192,1024]{1,0:T(8,128)S(1)}, f32[192,1024]{1,0:T(8,128)}, u32[]{:S(2)}) copy-start(f32[192,1024]{1,0:T(8,128)} %get-tuple-element.225.moment_ref) | copy-start | bytes 2359300
  671.7 25.6 %copy-start.36 = (f32[512,1536]{1,0:T(8,128)S(1)}, f32[512,1536]{1,0:T(8,128)}, u32[]{:S(2)}) copy-start(f32[512,1536]{1,0:T(8,128)} %copy-done.35) | copy-start | bytes 9437188
  671.7 25.6 %copy-start.38 = (f32[512,1536]{1,0:T(8,128)S(1)}, f32[512,1536]{1,0:T(8,128)}, u32[]{:S(2)}) copy-start(f32[512,1536]{1,0:T(8,128)} %copy-done.37) | copy-start | bytes 9437188
  671.7 25.6 %copy-start.45 = (bf16[1,2,512,1536]{3,2,1,0:T(8,128)(2,1)S(1)}, bf16[1,2,512,1536]{3,2,1,0:T(8,128)(2,1)}, u32[]{:S(2)}) copy-start(bf16[1,2,512,1536]{3,2,1,0:T(8,128)(2,1)} %param.24) | copy-start | bytes 9437188
  671.7 25.6 %copy-start.51 = (bf16[512,1536]{1,0:T(8,128)(2,1)S(1)}, bf16[512,1536]{1,0:T(8,128)(2,1)}, u32[]{:S(2)}) copy-start(bf16[512,1536]{1,0:T(8,128)(2,1)} %get-tuple-element.57) | copy-start | bytes 4718596
  671.7 25.6 %copy-start.52 = (bf16[512,1536]{1,0:T(8,128)(2,1)S(1)}, bf16[512,1536]{1,0:T(8,128)(2,1)}, u32[]{:S(2)}) copy-start(bf16[512,1536]{1,0:T(8,128)(2,1)} %get-tuple-element.59) | copy-start | bytes 4718596
  702.4 12.5 %copy-start.11 = (bf16[1536,512]{1,0:T(8,128)(2,1)S(1)}, bf16[1536,512]{1,0:T(8,128)(2,1)}, u32[]{:S(2)}) copy-start(bf16[1536,512]{1,0:T(8,128)(2,1)} %get-tuple-element.95) | copy-start | bytes 4718596
  702.4 12.5 %copy-start.27 = (f32[192,1024]{1,0:T(8,128)S(1)}, f32[192,1024]{1,0:T(8,128)}, u32[]{:S(2)}) copy-start(f32[192,1024]{1,0:T(8,128)} %get-tuple-element.224.moment_ref) | copy-start | bytes 2359300
  743.9 6.0 copy-start.10
  (91 other events, 288.3 us)
Sparse Core Ops, SparseCore 0:
  9.6 92.0 all-gather.3
  103.3 35.4 all-gather.5
  140.4 35.8 all-gather.7
  362.3 68.1 all-reduce.2
  645.0 67.7 all-reduce.4
